TPU v7x, 128 devices: a whole 4x4x4 slice. The times are simulated.
128 devices in a mesh: bank: 8 (over x, core), lane: 16 (over z, y).
Axes of the slice: x: 4, y: 4, z: 4, core: 2. Of those that a mesh axis runs over, the one named last changes fastest.
Arguments:
- amplitudes: float32 [2, 2048, 128, 128], P(None, ('bank', 'lane')), may hold values from -6 to 6
- energies: float32 [2048, 128, 128], P(('bank', 'lane')), may hold values from -2 to 2
- diagonal_angles: float32 [2, 128], replicated, may hold values from 0.3 to 1.2
- turn_angles: float32 [2, 4], replicated, may hold values from 0.3 to 1.2
Outputs:
- state_after: float32 [2, 2048, 128, 128], P(None, ('bank', 'lane'))
All inputs are finite; a program needn't handle non-finite values.
Results may differ from a plain program's by a relative error of at most 0.0003.
Values sent between devices are 32-bit elements; how exact they have to be, the bound alone decides.
No kernel may reach another device: no remote copies, remote signals or barrier semaphores. Data moves between devices by JAX's collectives and lax.ppermute only.
A program may use at most 64 MiB of HBM per device.

v0:
```python
import jax
import jax.numpy as jnp
from jax import lax
from jax.sharding import Mesh
from jax.sharding import PartitionSpec as P

LAYERS = 2
BANK = ("bank_0", "bank_1")
BANK_LANE = ("bank_0", "bank_1", "lane")


def split_up(shard, dim, peers):
    before, after = (shard.shape[:dim], shard.shape[dim + 1 :])
    return jnp.moveaxis(shard.reshape(*before, peers, -1, *after), dim, 0)


def in_order(tiles, dim):
    lengths = list(tiles.shape[1:])
    lengths[dim] *= tiles.shape[0]
    return jnp.moveaxis(tiles, 0, dim).reshape(lengths)


def moved_by_axis(tiles, axes, order):
    inside = tiles.shape[1:]
    filled = tiles.reshape(*(lax.axis_size(a) for a in axes), *inside)
    for k in order:
        filled = lax.all_to_all(filled, axes[k], k, k, tiled=True)
    return filled.reshape(-1, *inside)


def core_and_chips(shard, groups, order, split_dim, concat_dim):
    peers = lax.axis_size(groups[0]) * lax.axis_size(groups[1])
    tiles = split_up(shard, split_dim, peers)
    return in_order(moved_by_axis(tiles, groups, order), concat_dim)


def count_bits(values, count):
    places = jnp.arange(count.bit_length() - 1, dtype=jnp.int32)
    return jnp.sum(values[..., None] >> places & 1, axis=-1)


def plane_table(count, angle):
    rank = jnp.arange(count, dtype=jnp.int32)
    apart = count_bits(rank[:, None] ^ rank[None, :], count)
    minus = count_bits(rank[:, None] & (rank[:, None] ^ rank[None, :]), count)
    bits = count.bit_length() - 1
    size = jnp.cos(angle) ** (bits - apart).astype(jnp.float32) * jnp.sin(angle) ** apart.astype(
        jnp.float32
    )
    return size * jnp.where(minus % 2 == 1, -1.0, 1.0).astype(jnp.float32)


def mix_dim(values, dim, angle):
    real_part = plane_table(values.shape[dim], angle)
    moved = jnp.tensordot(values, real_part, axes=([dim], [0]), precision=lax.Precision.HIGHEST)
    return jnp.moveaxis(moved, -1, dim)


def phase_step(values, levels, angle):
    turn = angle * levels
    return jnp.stack(
        [
            values[0] * jnp.cos(turn) + values[1] * jnp.sin(turn),
            values[1] * jnp.cos(turn) - values[0] * jnp.sin(turn),
        ]
    )


def body(amplitudes, energies, diagonal_angles, turn_angles):
    values = amplitudes
    for layer in range(LAYERS):
        values = phase_step(values, energies, diagonal_angles[layer])
        values = mix_dim(values, 3, turn_angles[layer, 0])
        values = mix_dim(values, 2, turn_angles[layer, 1])
        moved = lax.all_to_all(values, BANK, split_axis=2, concat_axis=1, tiled=True)
        moved = mix_dim(moved, 1, turn_angles[layer, 2])
        values = core_and_chips(moved, ("bank_0", "bank_1"), (1, 0), 1, 2)
        moved = lax.all_to_all(values, "lane", split_axis=3, concat_axis=1, tiled=True)
        spread = moved.reshape(2, lax.axis_size("lane"), -1, moved.shape[2], moved.shape[3])
        moved = mix_dim(spread, 1, turn_angles[layer, 3]).reshape(moved.shape)
        values = lax.all_to_all(moved, "lane", split_axis=1, concat_axis=3, tiled=True)
    return values


def solution(mesh):
    torus = Mesh(mesh.devices.reshape(4, 2, mesh.shape["lane"]), ("bank_0", "bank_1", "lane"))
    in_specs = (P(None, BANK_LANE, None, None), P(BANK_LANE, None, None), P(), P())
    out_specs = P(None, BANK_LANE, None, None)
    return jax.shard_map(body, mesh=torus, in_specs=in_specs, out_specs=out_specs, check_vma=False)
```

profile of v0, /device:TPU:1, one launch (start us, length us, event | category | flops | bytes accessed | tf_op | source)
XLA Modules:
  0.0 325.4 jit_solution(13171402460288628376)
XLA Ops:
  0.0 1.6 fusion.163
  5.5 5.2 %fusion.21 = (f32[1,16,128,128]{3,2,1,0:T(8,128)S(1)}, f32[1,16,128,128]{3,2,1,0:T(8,128)S(1)}) fusion(f32[2,16,128,128]{3,2,1,0:T(8,128)} %param.4, f32[16,128,128]{2,1,0:T(8,128)} %param.5, f32[128]{0:T(128)S(1)} %get-tuple-element.20), kind=kLoop, calls=%fused_computation.22 | loop fusion | flops 1835008 | bytes 5243392 | tf_op jit(solution)/shard_map/stack | solution.py:61
  10.7 2.3 fusion
  12.9 2.0 convolution_bitcast_fusion.1
  14.9 2.0 copy.105
  16.9 5.8 %all-to-all-start = ((f32[2,16,128,128]{3,1,0,2:T(8,128)}), f32[2,16,128,128]{3,1,0,2:T(8,128)S(1)}, u32[]{:S(2)}, u32[]{:S(2)}) async-start(f32[2,16,128,128]{3,1,0,2:T(8,128)} %copy.105), calls=%async_computation | async-start | bytes 4194304 | tf_op jit(solution)/shard_map/all_to_all | solution.py:75
  24.1 24.8 %all-to-all-done = f32[2,16,128,128]{3,1,0,2:T(8,128)S(1)} async-done(((f32[2,16,128,128]{3,1,0,2:T(8,128)}), f32[2,16,128,128]{3,1,0,2:T(8,128)S(1)}, u32[]{:S(2)}, u32[]{:S(2)}) %all-to-all-start) | async-done | bytes 2097184 | tf_op jit(solution)/shard_map/all_to_all | solution.py:75
  49.1 2.2 fusion.31
  52.5 6.0 %all_to_all.119 = f32[4,2,2,16,16,128]{5,4,0,3,2,1:T(8,128)S(1)} all-to-all(f32[4,2,2,16,16,128]{5,4,0,3,2,1:T(8,128)S(1)} %copy.110), channel_id=1, replica_groups=mesh['bank_0'=4,'bank_1'=2,'lane'=16] {'bank_1'}, dimensions={1} | all-to-all | bytes 4194304 | tf_op jit(solution)/shard_map/all_to_all | solution.py:27
  58.9 28.5 %all_to_all.120 = f32[4,2,2,16,16,128]{5,4,1,3,2,0:T(8,128)S(1)} all-to-all(f32[4,2,2,16,16,128]{5,4,1,3,2,0:T(8,128)S(1)} %copy.111), channel_id=1, replica_groups=mesh['bank_0'=4,'bank_1'=2,'lane'=16] {'bank_0'}, dimensions={0} | all-to-all | bytes 4194304 | tf_op jit(solution)/shard_map/all_to_all | solution.py:27
  87.6 2.0 copy.113
  89.5 7.8 %all-to-all-start.3 = ((f32[2,16,128,128]{2,1,0,3:T(8,128)}), f32[2,16,128,128]{2,1,0,3:T(8,128)S(1)}, u32[]{:S(2)}, u32[]{:S(2)}) async-start(f32[2,16,128,128]{2,1,0,3:T(8,128)} %copy.113), calls=%async_computation.3 | async-start | bytes 4194304 | tf_op jit(solution)/shard_map/all_to_all | solution.py:78
  98.9 27.5 %all-to-all-done.3 = f32[2,16,128,128]{2,1,0,3:T(8,128)S(1)} async-done(((f32[2,16,128,128]{2,1,0,3:T(8,128)}), f32[2,16,128,128]{2,1,0,3:T(8,128)S(1)}, u32[]{:S(2)}, u32[]{:S(2)}) %all-to-all-start.3) | async-done | bytes 2097184 | tf_op jit(solution)/shard_map/all_to_all | solution.py:78
  126.4 3.6 %fusion.14 = f32[2,16,16,128,8]{3,1,4,2,0:T(8,128)S(1)} fusion(f32[2,16,128,16,8]{2,1,0,4,3:T(8,128)S(1)} %bitcast.151, s32[16,16]{1,0:T(8,128)S(1)} %get-tuple-element.22, f32[]{:T(128)} %bitcast.32, f32[]{:T(128)} %bitcast.31, s32[16,16]{1,0:T(8,128)S(1)} %get-tuple-element.21), kind=kOutput, calls=%fused_computation.15 | convolution fusion | flops 100667904 | bytes 4196360 | tf_op jit(solution)/shard_map/dot_general | solution.py:55
  130.6 1.5 copy.118
  132.1 5.2 %all-to-all-start.4 = ((f32[2,256,128,8]{2,3,0,1:T(8,128)}), f32[2,256,128,8]{2,3,0,1:T(8,128)S(1)}, u32[]{:S(2)}, u32[]{:S(2)}) async-start(f32[2,256,128,8]{2,3,0,1:T(8,128)} %copy.118), calls=%async_computation.4 | async-start | bytes 4194304 | tf_op jit(solution)/shard_map/all_to_all | solution.py:81
  140.1 27.1 %all-to-all-done.4 = f32[2,256,128,8]{2,3,0,1:T(8,128)S(1)} async-done(((f32[2,256,128,8]{2,3,0,1:T(8,128)}), f32[2,256,128,8]{2,3,0,1:T(8,128)S(1)}, u32[]{:S(2)}, u32[]{:S(2)}) %all-to-all-start.4) | async-done | bytes 2097184 | tf_op jit(solution)/shard_map/all_to_all | solution.py:81
  168.4 6.2 %add_bitcast_fusion = (f32[1,16,128,128]{3,2,1,0:T(8,128)S(1)}, f32[1,16,128,128]{3,2,1,0:T(8,128)S(1)}) fusion(f32[16,128,128]{2,1,0:T(8,128)S(1)} %copy.123, f32[16,128,128]{2,1,0:T(8,128)S(1)} %copy.121, f32[16,128,128]{2,1,0:T(8,128)} %param.5, f32[128]{0:T(128)S(1)} %get-tuple-element.19), kind=kLoop, calls=%fused_computation.30 | loop fusion | flops 1835008 | bytes 5243392 | tf_op jit(solution)/shard_map/stack | solution.py:61
  174.6 2.3 fusion.4
  176.8 2.0 convolution_bitcast_fusion
  178.8 2.0 copy.127
  180.8 5.9 %all-to-all-start.5 = ((f32[2,16,128,128]{3,1,0,2:T(8,128)}), f32[2,16,128,128]{3,1,0,2:T(8,128)S(1)}, u32[]{:S(2)}, u32[]{:S(2)}) async-start(f32[2,16,128,128]{3,1,0,2:T(8,128)} %copy.127), calls=%async_computation.5 | async-start | bytes 4194304 | tf_op jit(solution)/shard_map/all_to_all | solution.py:75
  188.0 25.0 %all-to-all-done.5 = f32[2,16,128,128]{3,1,0,2:T(8,128)S(1)} async-done(((f32[2,16,128,128]{3,1,0,2:T(8,128)}), f32[2,16,128,128]{3,1,0,2:T(8,128)S(1)}, u32[]{:S(2)}, u32[]{:S(2)}) %all-to-all-start.5) | async-done | bytes 2097184 | tf_op jit(solution)/shard_map/all_to_all | solution.py:75
  213.2 2.2 fusion.38
  216.6 6.0 %all_to_all.121 = f32[4,2,2,16,16,128]{5,4,0,3,2,1:T(8,128)S(1)} all-to-all(f32[4,2,2,16,16,128]{5,4,0,3,2,1:T(8,128)S(1)} %copy.132), channel_id=1, replica_groups=mesh['bank_0'=4,'bank_1'=2,'lane'=16] {'bank_1'}, dimensions={1} | all-to-all | bytes 4194304 | tf_op jit(solution)/shard_map/all_to_all | solution.py:27
  222.9 28.5 %all_to_all.122 = f32[4,2,2,16,16,128]{5,4,1,3,2,0:T(8,128)S(1)} all-to-all(f32[4,2,2,16,16,128]{5,4,1,3,2,0:T(8,128)S(1)} %copy.133), channel_id=1, replica_groups=mesh['bank_0'=4,'bank_1'=2,'lane'=16] {'bank_0'}, dimensions={0} | all-to-all | bytes 4194304 | tf_op jit(solution)/shard_map/all_to_all | solution.py:27
  251.6 2.0 copy.135
  253.6 3.7 %all-to-all-start.8 = ((f32[2,16,128,128]{2,1,0,3:T(8,128)}), f32[2,16,128,128]{2,1,0,3:T(8,128)S(1)}, u32[]{:S(2)}, u32[]{:S(2)}) async-start(f32[2,16,128,128]{2,1,0,3:T(8,128)} %copy.135), calls=%async_computation.8 | async-start | bytes 4194304 | tf_op jit(solution)/shard_map/all_to_all | solution.py:78
  258.7 28.5 %all-to-all-done.8 = f32[2,16,128,128]{2,1,0,3:T(8,128)S(1)} async-done(((f32[2,16,128,128]{2,1,0,3:T(8,128)}), f32[2,16,128,128]{2,1,0,3:T(8,128)S(1)}, u32[]{:S(2)}, u32[]{:S(2)}) %all-to-all-start.8) | async-done | bytes 2097184 | tf_op jit(solution)/shard_map/all_to_all | solution.py:78
  287.2 3.6 %fusion.17 = f32[2,16,16,128,8]{3,1,4,2,0:T(8,128)S(1)} fusion(f32[2,16,128,16,8]{2,1,0,4,3:T(8,128)S(1)} %bitcast.152, s32[16,16]{1,0:T(8,128)S(1)} %get-tuple-element.22, f32[]{:T(128)} %bitcast.71, f32[]{:T(128)} %bitcast.70, s32[16,16]{1,0:T(8,128)S(1)} %get-tuple-element.21), kind=kOutput, calls=%fused_computation.16 | convolution fusion | flops 100667904 | bytes 4196360 | tf_op jit(solution)/shard_map/dot_general | solution.py:55
  291.6 31.8 %all_to_all.123 = f32[2,256,128,8]{2,3,0,1:T(8,128)S(1)} all-to-all(f32[2,256,128,8]{2,3,0,1:T(8,128)S(1)} %copy.140), channel_id=1, replica_groups=mesh['bank_0'=4,'bank_1'=2,'lane'=16] {'lane'}, dimensions={1} | all-to-all | bytes 4194304 | tf_op jit(solution)/shard_map/all_to_all | solution.py:81
  323.6 1.8 copy.143
  (27 shorter events, 7.7 us)
Async XLA Ops:
  16.9 32.0 %all-to-all-start = ((f32[2,16,128,128]{3,1,0,2:T(8,128)}), f32[2,16,128,128]{3,1,0,2:T(8,128)S(1)}, u32[]{:S(2)}, u32[]{:S(2)}) async-start(f32[2,16,128,128]{3,1,0,2:T(8,128)} %copy.105), calls=%async_computation | async-start | bytes 4194304 | tf_op jit(solution)/shard_map/all_to_all | solution.py:75
  89.5 36.9 %all-to-all-start.3 = ((f32[2,16,128,128]{2,1,0,3:T(8,128)}), f32[2,16,128,128]{2,1,0,3:T(8,128)S(1)}, u32[]{:S(2)}, u32[]{:S(2)}) async-start(f32[2,16,128,128]{2,1,0,3:T(8,128)} %copy.113), calls=%async_computation.3 | async-start | bytes 4194304 | tf_op jit(solution)/shard_map/all_to_all | solution.py:78
  132.1 35.1 %all-to-all-start.4 = ((f32[2,256,128,8]{2,3,0,1:T(8,128)}), f32[2,256,128,8]{2,3,0,1:T(8,128)S(1)}, u32[]{:S(2)}, u32[]{:S(2)}) async-start(f32[2,256,128,8]{2,3,0,1:T(8,128)} %copy.118), calls=%async_computation.4 | async-start | bytes 4194304 | tf_op jit(solution)/shard_map/all_to_all | solution.py:81
  180.8 32.1 %all-to-all-start.5 = ((f32[2,16,128,128]{3,1,0,2:T(8,128)}), f32[2,16,128,128]{3,1,0,2:T(8,128)S(1)}, u32[]{:S(2)}, u32[]{:S(2)}) async-start(f32[2,16,128,128]{3,1,0,2:T(8,128)} %copy.127), calls=%async_computation.5 | async-start | bytes 4194304 | tf_op jit(solution)/shard_map/all_to_all | solution.py:75
  253.6 33.6 %all-to-all-start.8 = ((f32[2,16,128,128]{2,1,0,3:T(8,128)}), f32[2,16,128,128]{2,1,0,3:T(8,128)S(1)}, u32[]{:S(2)}, u32[]{:S(2)}) async-start(f32[2,16,128,128]{2,1,0,3:T(8,128)} %copy.135), calls=%async_computation.8 | async-start | bytes 4194304 | tf_op jit(solution)/shard_map/all_to_all | solution.py:78
where the time goes:
time: 327 us; the launch traced here: 325 us
  waiting for transfers between devices  133 us (41%)
  blocking collectives  101 us (31%)
  starting transfers between devices  28.4 us (9%)
  local copies, waits for them, and re-layouts  20.3 us (6%)
  matrix products  20 us (6%)
  other arithmetic  11.5 us (4%)
  between operations  11.5 us (4%)
    all_to_all x4, blocking collectives, moved_by_axis(): filled = lax.all_to_all(filled, axes[k], k, k, tiled=True)  69.1 us
    all_to_all x2, waiting for transfers between devices, body(): lax.all_to_all(values, 'lane', split_axis=3, concat_axis=1, tiled=True)  56 us
    all_to_all x2, waiting for transfers between devices, body(): lax.all_to_all(values, BANK, split_axis=2, concat_axis=1, tiled=True)  49.8 us
    all_to_all x1, blocking collectives, body(): lax.all_to_all(moved, 'lane', split_axis=1, concat_axis=3, tiled=True)  31.8 us
    all_to_all x1, waiting for transfers between devices, body(): lax.all_to_all(moved, 'lane', split_axis=1, concat_axis=3, tiled=True)  27.1 us
    dot_general x8, matrix products, mix_dim(): jnp.tensordot(values, real_part, axes=([dim], [0]), precision=lax.Precisi...  20 us
    all_to_all x2, starting transfers between devices, body(): lax.all_to_all(values, BANK, split_axis=2, concat_axis=1, tiled=True)  11.7 us
    all_to_all x2, starting transfers between devices, body(): lax.all_to_all(values, 'lane', split_axis=3, concat_axis=1, tiled=True)  11.5 us
  transfers between devices with their start and end apart: 5, of which 5 were waited for; matrix products, arithmetic and copies ran while one was open for 0% of the time, Pallas kernels for 0%

commit v1 on v0

v1 whole, which is shorter than its diff:
```python
import functools

import jax
import jax.numpy as jnp
import numpy as np
from jax import lax
from jax.experimental import pallas as pl
from jax.experimental.pallas import tpu as pltpu
from jax.sharding import Mesh
from jax.sharding import PartitionSpec as P

AXES = ("x", "c", "z", "y")
XZY = ("x", "z", "y")
VMEM = pltpu.VMEM
SMEM = pltpu.SMEM
TILES = 256
COS0, SIN0, SCALE, TAN1, TAN2, TAN3, TANC = range(7)


def fit(fn, terms, most=5.77):
    k = np.arange(400)
    s = most / 2 * (1 + np.cos(np.pi * (k + 0.5) / 400))
    series = np.polynomial.Chebyshev.fit(s, fn(np.sqrt(s)), terms - 1, domain=[0, most])
    return [float(c) for c in series.convert(kind=np.polynomial.Polynomial).coef]


COS = fit(np.cos, 8)
SIN = fit(lambda t: np.sinc(t / np.pi), 7)


def horner(coef, s):
    total = s * coef[-1] + coef[-2]
    for c in coef[-3::-1]:
        total = total * s + c
    return total


def phase(re, im, level, angle):
    turn = level * angle
    square = turn * turn
    cos = horner(COS, square)
    sin = horner(SIN, square) * turn
    return re * cos + im * sin, im * cos - re * sin


def rotate(tiles, bit, tan):
    step = 1 << bit
    out = list(tiles)
    for i, u in enumerate(tiles):
        if not i & step:
            v = tiles[i + step]
            out[i] = u - tan * v
            out[i + step] = v + tan * u
    return out


def rotate_sublanes(tiles, tan):
    place = lax.broadcasted_iota(jnp.int32, (8, 128), 0)
    for bit in range(3):
        step = 1 << bit
        one = (place & step) != 0
        weight = jnp.where(one, tan, -tan)
        out = []
        for t in tiles:
            below = pltpu.roll(t, step, 0)
            if step == 4:
                other = below
            else:
                other = jnp.where(one, below, pltpu.roll(t, 8 - step, 0))
            out.append(t + weight * other)
        tiles = out
    return tiles


def lane_table(scalars, layer):
    row = lax.broadcasted_iota(jnp.int32, (128, 128), 0)
    col = lax.broadcasted_iota(jnp.int32, (128, 128), 1)
    cos, sin = scalars[layer, COS0], scalars[layer, SIN0]
    table = jnp.full((128, 128), scalars[layer, SCALE], jnp.float32)
    for bit in range(7):
        a, b = (row >> bit) & 1, (col >> bit) & 1
        table = table * jnp.where(a == b, cos, jnp.where(b == 1, sin, -sin))
    high = table.astype(jnp.bfloat16)
    low = (table - high.astype(jnp.float32)).astype(jnp.bfloat16)
    return high, low


def store_table(scalars, layer, table_ref):
    high, low = lane_table(scalars, layer)
    table_ref[0:128, 0:128] = high
    table_ref[0:128, 128:256] = low
    table_ref[128:256, 0:128] = high
    table_ref[128:256, 128:256] = jnp.zeros_like(high)


def mix_lanes(tiles, table_ref):
    rows = jnp.concatenate(tiles, axis=0)
    high = rows.astype(jnp.bfloat16)
    low = (rows - high.astype(jnp.float32)).astype(jnp.bfloat16)
    both = jnp.dot(
        jnp.concatenate([high, low], axis=1), table_ref[...], preferred_element_type=jnp.float32
    )
    mixed = both[:, 0:128] + both[:, 128:256]
    return [mixed[8 * i : 8 * i + 8] for i in range(len(tiles))]


def first_kernel(scalars, state, levels, angle, out):
    tan = scalars[0, TAN2]

    @pl.loop(0, 32)
    def _(j):
        re, im = [], []
        for i in range(8):
            a, b = phase(state[0, 32 * i + j], state[1, 32 * i + j], levels[32 * i + j], angle[...])
            re.append(a)
            im.append(b)
        for p, tiles in enumerate((re, im)):
            for bit in range(3):
                tiles = rotate(tiles, bit, tan)
            for i in range(8):
                out[p, 32 * i + j] = tiles[i]


def second_kernel(scalars, own, other, out, table_ref):
    store_table(scalars, 0, table_ref)
    tan_core, tan_row, tan_block = scalars[0, TANC], scalars[0, TAN1], scalars[0, TAN2]

    @pl.loop(0, 8)
    def _(b):
        for p in range(2):
            tiles = [own[p, 32 * b + i] + tan_core * other[p, 32 * b + i] for i in range(32)]
            tiles = mix_lanes(tiles, table_ref)
            for bit, tan in ((4, tan_block), (3, tan_row), (2, tan_row), (1, tan_row), (0, tan_row)):
                tiles = rotate(tiles, bit, tan)
            tiles = rotate_sublanes(tiles, tan_row)
            for i in range(32):
                out[8 * b + i // 4, p, i % 4] = tiles[i]


def third_kernel(scalars, state, levels, angle, out, table_ref, held):
    store_table(scalars, 1, table_ref)
    x0, zy0 = scalars[0, TAN2], scalars[0, TAN3]
    zy1, row1 = scalars[1, TAN3], scalars[1, TAN1]

    @pl.loop(0, 8)
    def _(g):
        for p in range(2):
            for r in range(4):
                tiles = [state[8 * i + g, p, r] for i in range(8)]
                for bit, tan in ((2, x0), (1, x0), (0, zy0)):
                    tiles = rotate(tiles, bit, tan)
                for i in range(8):
                    held[p, 32 * i + 4 * g + r] = tiles[i]

    @pl.loop(0, 8)
    def _(b):
        parts = [[None] * 32, [None] * 32]
        for r in range(4):
            two = []
            for p in range(2):
                tiles = [held[p, 32 * b + 4 * i + r] for i in range(8)]
                for bit in range(3):
                    tiles = rotate(tiles, bit, zy0)
                two.append(tiles)
            for i in range(8):
                level = levels[32 * b + 4 * i + r]
                parts[0][4 * i + r], parts[1][4 * i + r] = phase(two[0][i], two[1][i], level, angle[...])
        for p in range(2):
            tiles = mix_lanes(parts[p], table_ref)
            for bit, tan in ((4, zy1), (3, zy1), (2, zy1), (1, row1), (0, row1)):
                tiles = rotate(tiles, bit, tan)
            tiles = rotate_sublanes(tiles, row1)
            for i in range(32):
                out[p, 32 * b + i] = tiles[i]


def fourth_kernel(scalars, own, other, out):
    core, x1, zy1 = scalars[1, TANC], scalars[1, TAN2], scalars[1, TAN3]

    @pl.loop(0, 8)
    def _(g):
        for p in range(2):
            for r in range(4):
                at = 4 * g + r
                tiles = [own[p, 32 * i + at] + core * other[p, 32 * i + at] for i in range(8)]
                for bit, tan in ((2, x1), (1, x1), (0, zy1)):
                    tiles = rotate(tiles, bit, tan)
                for i in range(8):
                    out[8 * i + g, p, r] = tiles[i]


def fifth_kernel(scalars, state, out, held):
    block, row = scalars[1, TAN2], scalars[1, TAN1]

    @pl.loop(0, 8)
    def _(g):
        for p in range(2):
            for r in range(4):
                tiles = [state[8 * i + g, p, r] for i in range(8)]
                for bit in range(3):
                    tiles = rotate(tiles, bit, block)
                for i in range(8):
                    held[p, 32 * i + 4 * g + r] = tiles[i]

    @pl.loop(0, 8)
    def _(b):
        for p in range(2):
            for r in range(4):
                tiles = [held[p, 32 * b + 4 * i + r] for i in range(8)]
                for bit, tan in ((2, block), (1, row), (0, row)):
                    tiles = rotate(tiles, bit, tan)
                for i in range(8):
                    out[p, 32 * b + 4 * i + r] = tiles[i]


HOME = (2, TILES, 8, 128)
AWAY = (64, 2, 4, 8, 128)


def call(kernel, name, shape, inputs, scratch=(), flops=20_000_000):
    spaces = [pl.BlockSpec(memory_space=SMEM)] + [pl.BlockSpec(memory_space=VMEM)] * (len(inputs) - 1)
    return pl.pallas_call(
        kernel,
        out_shape=jax.ShapeDtypeStruct(shape, jnp.float32),
        in_specs=spaces,
        out_specs=pl.BlockSpec(memory_space=VMEM),
        scratch_shapes=list(scratch),
        name=name,
        cost_estimate=pl.CostEstimate(flops=flops, bytes_accessed=5 << 20, transcendentals=0),
        compiler_params=pltpu.CompilerParams(vmem_limit_bytes=24 << 20),
    )(*inputs)


def swap_core(state):
    return lax.ppermute(state, "c", [(0, 1), (1, 0)])


def exchange(state):
    return lax.all_to_all(state, XZY, 0, 0, tiled=True)


def layer_scalars(turn_angles):
    cos, sin = jnp.cos(turn_angles), jnp.sin(turn_angles)
    tan = sin / cos
    scale = (cos[:, 1] * cos[:, 2]) ** 7 * cos[:, 3] ** 4
    core = jnp.where(lax.axis_index("c") == 1, tan[:, 2], -tan[:, 2])
    return jnp.stack([cos[:, 0], sin[:, 0], scale, tan[:, 1], tan[:, 2], tan[:, 3], core, core], axis=1)


def body(amplitudes, energies, diagonal_angles, turn_angles):
    scalars = layer_scalars(turn_angles)
    state = amplitudes.reshape(HOME)
    levels = energies.reshape(TILES, 8, 128)
    away_levels = exchange(energies.reshape(64, 32, 128)).reshape(TILES, 8, 128)
    table = pltpu.VMEM((256, 256), jnp.bfloat16)
    held = pltpu.VMEM(HOME, jnp.float32)
    state = call(first_kernel, "first", HOME, (scalars, state, levels, diagonal_angles[0:1]))
    state = call(second_kernel, "second", AWAY, (scalars, state, swap_core(state)), (table,))
    state = exchange(state.reshape(64, 2, 32, 128)).reshape(AWAY)
    state = call(
        third_kernel, "third", HOME, (scalars, state, away_levels, diagonal_angles[1:2]), (table, held)
    )
    state = call(fourth_kernel, "fourth", AWAY, (scalars, state, swap_core(state)))
    state = exchange(state.reshape(64, 2, 32, 128)).reshape(AWAY)
    state = call(fifth_kernel, "fifth", HOME, (scalars, state), (held,))
    return state.reshape(amplitudes.shape)


def solution(mesh):
    torus = Mesh(mesh.devices.reshape(4, 2, 4, 4), AXES)
    in_specs = (P(None, AXES, None, None), P(AXES, None, None), P(), P())
    out_specs = P(None, AXES, None, None)
    return jax.shard_map(body, mesh=torus, in_specs=in_specs, out_specs=out_specs, check_vma=False)
```

time: 327 us -> 120 us (0.37)
  waiting for transfers between devices: 133 us -> 14.9 us
  blocking collectives: 101 us -> 64 us
  matrix products: 20 us -> 0 us
  Pallas kernels: 0 us -> 17.4 us
  local copies, waits for them, and re-layouts: 20.3 us -> 4.56 us
  starting transfers between devices: 28.4 us -> 16.8 us
  between operations: 11.5 us -> 0.06 us
  other arithmetic: 11.5 us -> 0.16 us
    all_to_all x5 -> x1, waiting for transfers between devices: 133 us -> 11.1 us  [exchange(): return lax.all_to_all(state, XZY, 0, 0, tiled=True)]
    all_to_all x5 -> x2, blocking collectives: 101 us -> 64 us  [exchange(): return lax.all_to_all(state, XZY, 0, 0, tiled=True)]
    dot_general x8 -> x0, matrix products: 20 us -> none  [mix_dim(): jnp.tensordot(values, real_part, axes=([dim], [0]), precision=lax.Precisi...]
    pallas_call x0 -> x5, Pallas kernels: none -> 17.4 us  [call(): pl.pallas_call(kernel, out_shape=jax.ShapeDtypeStruct(shape, jnp.float32)...]
    all_to_all x5 -> x1, starting transfers between devices: 28.4 us -> 11.2 us  [exchange(): return lax.all_to_all(state, XZY, 0, 0, tiled=True)]
    another operation x2 -> x0, other arithmetic: 11.3 us -> none  [phase_step(): jnp.stack([values[0] * jnp.cos(turn) + values[1] * jnp.sin(turn), values[...]
    reshape x6 -> x0, local copies, waits for them, and re-layouts: 8.02 us -> none  [the longest x2 3.93 us: in_order(): return jnp.moveaxis(tiles, 0, dim).reshape(lengths)]
    ppermute x0 -> x2, starting transfers between devices: none -> 5.52 us  [swap_core(): return lax.ppermute(state, 'c', [(0, 1), (1, 0)])]
  transfers between devices with their start and end apart: 5 -> 3, of which waited for: 5 -> 2; matrix products, arithmetic and copies ran while one was open for 0% -> 0% of each run, Pallas kernels for 0% -> 4%
where the time goes in v1:
time: 120 us; the launch traced here: 118 us
  blocking collectives  64 us (53%)
  Pallas kernels  17.4 us (14%)
  starting transfers between devices  16.8 us (14%)
  waiting for transfers between devices  14.9 us (12%)
  local copies, waits for them, and re-layouts  4.56 us (4%)
    all_to_all x2, blocking collectives, exchange(): return lax.all_to_all(state, XZY, 0, 0, tiled=True)  64 us
    pallas_call x5, Pallas kernels, call(): pl.pallas_call(kernel, out_shape=jax.ShapeDtypeStruct(shape, jnp.float32)...  17.4 us
    all_to_all x1, starting transfers between devices, exchange(): return lax.all_to_all(state, XZY, 0, 0, tiled=True)  11.2 us
    all_to_all x1, waiting for transfers between devices, exchange(): return lax.all_to_all(state, XZY, 0, 0, tiled=True)  11.1 us
    ppermute x2, starting transfers between devices, swap_core(): return lax.ppermute(state, 'c', [(0, 1), (1, 0)])  5.52 us
    ppermute x2, waiting for transfers between devices, swap_core(): return lax.ppermute(state, 'c', [(0, 1), (1, 0)])  3.79 us
    unnamed x4, local copies, waits for them, and re-layouts  2.91 us
  transfers between devices with their start and end apart: 3, of which 2 were waited for; matrix products, arithmetic and copies ran while one was open for 0% of the time, Pallas kernels for 4%

profile of v1, /device:TPU:1, one launch (start us, length us, event | category | flops | bytes accessed | tf_op | source)
XLA Modules:
  0.0 117.8 jit_solution(2753429418799153061)
XLA Ops:
  0.0 0.7 fusion.3
  0.7 0.1 fusion.1
  0.8 0.1 slice.36
  0.9 0.1 negate_select_fusion
  1.0 0.8 fusion.2
  1.7 0.1 stack.2.scalars
  1.8 0.0 copy-start.1
  1.8 1.6 %copy-done.1 = f32[2,16,128,128]{3,2,1,0:T(8,128)S(1)} copy-done((f32[2,16,128,128]{3,2,1,0:T(8,128)S(1)}, f32[2,16,128,128]{3,2,1,0:T(8,128)}, u32[]{:S(2)}) %copy-start.1) | copy-done | bytes 2097176
  3.4 3.0 %first.1.own = f32[2,256,8,128]{3,2,1,0:T(8,128)S(1)} custom-call(f32[2,8]{1,0:T(2,128)S(1)} %stack.2.scalars, f32[2,256,8,128]{3,2,1,0:T(8,128)S(1)} %bitcast.15, f32[256,8,128]{2,1,0:T(8,128)} %bitcast.1.levels, f32[1,128]{1,0:T(1,128)S(1)} %get-tuple-element.6.angle), custom_call_target="tpu_custom_call" | custom-call | flops 20000000 | bytes 5242880 | tf_op jit(solution)/shard_map/first/pallas_call | solution.py:222
  6.4 1.5 %collective-permute-start = (f32[2,256,8,128]{3,2,1,0:T(8,128)S(1)}, f32[2,256,8,128]{3,2,1,0:T(8,128)}, u32[]{:S(2)}, u32[]{:S(2)}) collective-permute-start(f32[2,256,8,128]{3,2,1,0:T(8,128)S(1)} %first.1.own), channel_id=1, source_target_pairs={{0,16},{16,0},{1,17},{17,1},{2,18},{18,2},{3,19},{19,3},{4,20},{20... | collective-permute-start | bytes 6291464 | tf_op jit(solution)/shard_map/ppermute | solution.py:235
  7.9 11.2 %all-to-all-start.1 = ((f32[64,32,128]{2,1,0:T(8,128)}), f32[64,32,128]{2,1,0:T(8,128)S(1)}, u32[]{:S(2)}, u32[]{:S(2)}) async-start(f32[64,32,128]{2,1,0:T(8,128)} %bitcast.4), calls=%async_computation.1 | async-start | bytes 2097152 | tf_op jit(solution)/shard_map/all_to_all | solution.py:239
  19.1 0.0 collective-permute-done.other
  19.1 5.0 %second.1 = f32[64,2,4,8,128]{4,3,2,1,0:T(8,128)S(1)} custom-call(f32[2,8]{1,0:T(2,128)S(1)} %stack.2.scalars, f32[2,256,8,128]{3,2,1,0:T(8,128)S(1)} %first.1.own, f32[2,256,8,128]{3,2,1,0:T(8,128)} %collective-permute-done.other), custom_call_target="tpu_custom_call" | custom-call | flops 20000000 | bytes 5242880 | tf_op jit(solution)/shard_map/second/pallas_call | solution.py:222
  24.1 0.0 copy-start
  24.1 1.3 %copy-done = f32[64,2,4,8,128]{4,3,2,1,0:T(8,128)} copy-done((f32[64,2,4,8,128]{4,3,2,1,0:T(8,128)}, f32[64,2,4,8,128]{4,3,2,1,0:T(8,128)S(1)}, u32[]{:S(2)}) %copy-start) | copy-done | bytes 2097176
  25.5 11.1 %all-to-all-done.1 = f32[64,32,128]{2,1,0:T(8,128)S(1)} async-done(((f32[64,32,128]{2,1,0:T(8,128)}), f32[64,32,128]{2,1,0:T(8,128)S(1)}, u32[]{:S(2)}, u32[]{:S(2)}) %all-to-all-start.1) | async-done | bytes 1048608 | tf_op jit(solution)/shard_map/all_to_all | solution.py:239
  36.5 32.7 %all_to_all.15 = f32[64,2,32,128]{3,2,1,0:T(8,128)S(1)} all-to-all(f32[64,2,32,128]{3,2,1,0:T(8,128)} %bitcast.11), channel_id=1, replica_groups=mesh['x'=4,'c'=2,'z'=4,'y'=4] {'x','z','y'}, dimensions={0} | all-to-all | bytes 4194304 | tf_op jit(solution)/shard_map/all_to_all | solution.py:239
  69.2 5.4 %third.1.own = f32[2,256,8,128]{3,2,1,0:T(8,128)S(1)} custom-call(f32[2,8]{1,0:T(2,128)S(1)} %stack.2.scalars, f32[64,2,4,8,128]{4,3,2,1,0:T(8,128)S(1)} %bitcast.12, f32[256,8,128]{2,1,0:T(8,128)S(1)} %bitcast.14, f32[1,128]{1,0:T(1,128)S(1)} %get-tuple-element.5.angle), custom_call_target="tpu_custom_call" | custom-call | flops 20000000 | bytes 5242880 | tf_op jit(solution)/shard_map/third/pallas_call | solution.py:222
  74.7 4.1 %collective-permute-start.1 = (f32[2,256,8,128]{3,2,1,0:T(8,128)S(1)}, f32[2,256,8,128]{3,2,1,0:T(8,128)S(1)}, u32[]{:S(2)}, u32[]{:S(2)}) collective-permute-start(f32[2,256,8,128]{3,2,1,0:T(8,128)S(1)} %third.1.own), channel_id=1, source_target_pairs={{0,16},{16,0},{1,17},{17,1},{2,18},{18,2},{3,19},{19,3},{4,20},{20... | collective-permute-start | bytes 6291464 | tf_op jit(solution)/shard_map/ppermute | solution.py:235
  78.7 3.8 %collective-permute-done.1.other = f32[2,256,8,128]{3,2,1,0:T(8,128)S(1)} collective-permute-done((f32[2,256,8,128]{3,2,1,0:T(8,128)S(1)}, f32[2,256,8,128]{3,2,1,0:T(8,128)S(1)}, u32[]{:S(2)}, u32[]{:S(2)}) %collective-permute-start.1) | collective-permute-done | bytes 2097184 | tf_op jit(solution)/shard_map/ppermute | solution.py:235
  82.5 1.2 %fourth.1 = f32[64,2,4,8,128]{4,3,2,1,0:T(8,128)S(1)} custom-call(f32[2,8]{1,0:T(2,128)S(1)} %stack.2.scalars, f32[2,256,8,128]{3,2,1,0:T(8,128)S(1)} %third.1.own, f32[2,256,8,128]{3,2,1,0:T(8,128)S(1)} %collective-permute-done.1.other), custom_call_target="tpu_custom_call" | custom-call | flops 20000000 | bytes 5242880 | tf_op jit(solution)/shard_map/fourth/pallas_call | solution.py:222
  83.7 31.3 %all_to_all.16 = f32[64,2,32,128]{3,2,1,0:T(8,128)S(1)} all-to-all(f32[64,2,32,128]{3,2,1,0:T(8,128)S(1)} %bitcast.13), channel_id=1, replica_groups=mesh['x'=4,'c'=2,'z'=4,'y'=4] {'x','z','y'}, dimensions={0} | all-to-all | bytes 4194304 | tf_op jit(solution)/shard_map/all_to_all | solution.py:239
  115.0 2.8 %fifth.1 = f32[2,256,8,128]{3,2,1,0:T(8,128)} custom-call(f32[2,8]{1,0:T(2,128)S(1)} %stack.2.scalars, f32[64,2,4,8,128]{4,3,2,1,0:T(8,128)S(1)} %bitcast.10), custom_call_target="tpu_custom_call" | custom-call | flops 20000000 | bytes 5242880 | tf_op jit(solution)/shard_map/fifth/pallas_call | solution.py:222
  (1 shorter events, 0.0 us)
Async XLA Ops:
  1.8 1.6 %copy-start.1 = (f32[2,16,128,128]{3,2,1,0:T(8,128)S(1)}, f32[2,16,128,128]{3,2,1,0:T(8,128)}, u32[]{:S(2)}) copy-start(f32[2,16,128,128]{3,2,1,0:T(8,128)} %param.4) | copy-start | bytes 6291460
  6.4 12.7 %collective-permute-start = (f32[2,256,8,128]{3,2,1,0:T(8,128)S(1)}, f32[2,256,8,128]{3,2,1,0:T(8,128)}, u32[]{:S(2)}, u32[]{:S(2)}) collective-permute-start(f32[2,256,8,128]{3,2,1,0:T(8,128)S(1)} %first.1.own), channel_id=1, source_target_pairs={{0,16},{16,0},{1,17},{17,1},{2,18},{18,2},{3,19},{19,3},{4,20},{20... | collective-permute-start | bytes 6291464 | tf_op jit(solution)/shard_map/ppermute | solution.py:235
  7.9 28.7 %all-to-all-start.1 = ((f32[64,32,128]{2,1,0:T(8,128)}), f32[64,32,128]{2,1,0:T(8,128)S(1)}, u32[]{:S(2)}, u32[]{:S(2)}) async-start(f32[64,32,128]{2,1,0:T(8,128)} %bitcast.4), calls=%async_computation.1 | async-start | bytes 2097152 | tf_op jit(solution)/shard_map/all_to_all | solution.py:239
  24.1 1.3 %copy-start = (f32[64,2,4,8,128]{4,3,2,1,0:T(8,128)}, f32[64,2,4,8,128]{4,3,2,1,0:T(8,128)S(1)}, u32[]{:S(2)}) copy-start(f32[64,2,4,8,128]{4,3,2,1,0:T(8,128)S(1)} %second.1) | copy-start | bytes 6291460
  74.7 7.8 %collective-permute-start.1 = (f32[2,256,8,128]{3,2,1,0:T(8,128)S(1)}, f32[2,256,8,128]{3,2,1,0:T(8,128)S(1)}, u32[]{:S(2)}, u32[]{:S(2)}) collective-permute-start(f32[2,256,8,128]{3,2,1,0:T(8,128)S(1)} %third.1.own), channel_id=1, source_target_pairs={{0,16},{16,0},{1,17},{17,1},{2,18},{18,2},{3,19},{19,3},{4,20},{20... | collective-permute-start | bytes 6291464 | tf_op jit(solution)/shard_map/ppermute | solution.py:235

commit v2 on v0

v2 whole, which is shorter than its diff:
```python
import jax
import jax.numpy as jnp
import numpy as np
from jax import lax
from jax.experimental import pallas as pl
from jax.experimental.pallas import tpu as pltpu
from jax.sharding import Mesh
from jax.sharding import PartitionSpec as P

AXES = ("x", "c", "z", "y")
ORDER = ("y", "z", "x", "c")
VMEM = pltpu.VMEM
SMEM = pltpu.SMEM
PIECES = 4
HOME = (2, 8, 32, 8, 128)
SENT = (8, 16, 3, 2, 8, 128)
AWAY = (8, 16, 2, 2, 8, 128)
ROW, BLOCK, MIDDLE = 0, 1, 2


def fit(fn, terms, most=5.77):
    k = np.arange(400)
    s = most / 2 * (1 + np.cos(np.pi * (k + 0.5) / 400))
    series = np.polynomial.Chebyshev.fit(s, fn(np.sqrt(s)), terms - 1, domain=[0, most])
    return [float(c) for c in series.convert(kind=np.polynomial.Polynomial).coef]


COS = fit(np.cos, 8)
SIN = fit(lambda t: np.sinc(t / np.pi), 7)


def horner(coef, s):
    total = s * coef[-1] + coef[-2]
    for c in coef[-3::-1]:
        total = total * s + c
    return total


def cos_sin(turn):
    square = turn * turn
    return horner(COS, square), horner(SIN, square) * turn


def phase(re, im, level, angle):
    cos, sin = cos_sin(level * angle)
    return re * cos + im * sin, im * cos - re * sin


def rotate(tiles, bit, tan):
    step = 1 << bit
    out = list(tiles)
    for i, u in enumerate(tiles):
        if not i & step:
            v = tiles[i + step]
            out[i] = u - tan * v
            out[i + step] = v + tan * u
    return out


def rotate_all(tiles, tans):
    for bit, tan in zip(reversed(range(len(tans))), tans):
        tiles = rotate(tiles, bit, tan)
    return tiles


def rotate_sublanes(tiles, tan):
    place = lax.broadcasted_iota(jnp.int32, (8, 128), 0)
    for bit in range(3):
        step = 1 << bit
        one = (place & step) != 0
        weight = jnp.where(one, tan, -tan)
        out = []
        for t in tiles:
            other = pltpu.roll(t, step, 0)
            if step < 4:
                other = jnp.where(one, other, pltpu.roll(t, 8 - step, 0))
            out.append(t + weight * other)
        tiles = out
    return tiles


def store_table(turn, layer, table_ref):
    cos, sin = [], []
    for g in range(4):
        c, s = cos_sin(jnp.full((8, 128), turn[layer, g], jnp.float32))
        cos.append(c)
        sin.append(s)
    pair = cos[1] * cos[2]
    cube = pair * pair * pair
    scale = cube * cube * pair * (cos[3] * cos[3]) * (cos[3] * cos[3])
    col = lax.broadcasted_iota(jnp.int32, (8, 128), 1)
    sub = lax.broadcasted_iota(jnp.int32, (8, 128), 0)
    for bit in range(3):
        a, b = (sub >> bit) & 1, (col >> bit) & 1
        scale = scale * jnp.where(a == b, cos[0], jnp.where(b == 1, sin[0], -sin[0]))
    for k in range(16):
        table = scale
        for bit in range(4):
            b = (col >> (bit + 3)) & 1
            if (k >> bit) & 1:
                table = table * jnp.where(b == 1, cos[0], -sin[0])
            else:
                table = table * jnp.where(b == 1, sin[0], cos[0])
        high = table.astype(jnp.bfloat16)
        low = (table - high.astype(jnp.float32)).astype(jnp.bfloat16)
        rows = slice(8 * k, 8 * k + 8)
        more = slice(128 + 8 * k, 136 + 8 * k)
        table_ref[rows, 0:128] = high
        table_ref[rows, 128:256] = low
        table_ref[more, 0:128] = high
        table_ref[more, 128:256] = jnp.zeros_like(high)
    return [sin[g] / cos[g] for g in (1, 2, 3)]


def mix_lanes(tiles, table_ref):
    rows = jnp.concatenate(tiles, axis=0)
    high = rows.astype(jnp.bfloat16)
    low = (rows - high.astype(jnp.float32)).astype(jnp.bfloat16)
    both = jnp.dot(
        jnp.concatenate([high, low], axis=1), table_ref[...], preferred_element_type=jnp.float32
    )
    mixed = both[:, 0:128] + both[:, 128:256]
    return [mixed[8 * i : 8 * i + 8] for i in range(len(tiles))]


def first_kernel(
    turn_hbm, angle_hbm, state_hbm, levels_hbm, out, tans, next_table, turn, angle, state, table, sems
):
    small = [
        pltpu.make_async_copy(turn_hbm, turn, sems.at[0]),
        pltpu.make_async_copy(angle_hbm, angle, sems.at[1]),
    ]
    copies = []
    for k in range(PIECES):
        js, qs = pl.ds(32 // PIECES * k, 32 // PIECES), pl.ds(16 // PIECES * k, 16 // PIECES)
        copies.append(
            (
                pltpu.make_async_copy(levels_hbm.at[:, qs], out.at[:, qs, 2], sems.at[2 + 2 * k]),
                pltpu.make_async_copy(state_hbm.at[:, :, js], state.at[:, :, js], sems.at[3 + 2 * k]),
            )
        )
    for c in small:
        c.start()
    for pair in copies:
        for c in pair:
            c.start()
    for c in small:
        c.wait()
    row0, block0, middle0 = store_table(turn, 0, table)
    later = store_table(turn, 1, next_table)
    for i, t in enumerate([row0, block0, middle0, *later]):
        tans[i] = t
    turned = jnp.broadcast_to(angle[0:1], (8, 128))

    for k in range(PIECES):
        for c in copies[k]:
            c.wait()

        @pl.loop(32 // PIECES * k, 32 // PIECES * (k + 1))
        def _(j):
            re, im = [], []
            for i in range(8):
                level = out[i, j >> 1, 2, j & 1]
                a, b = phase(state[0, i, j], state[1, i, j], level, turned)
                re.append(a)
                im.append(b)
            for p, tiles in enumerate((re, im)):
                tiles = rotate_all(tiles, [block0] * 3)
                for i in range(8):
                    state[p, i, j] = tiles[i]

    @pl.loop(0, 8)
    def _(b):
        for p in range(2):
            tiles = mix_lanes([state[p, b, i] for i in range(32)], table)
            tiles = rotate_all(tiles, [block0, row0, row0, row0, row0])
            tiles = rotate_sublanes(tiles, row0)
            for i in range(32):
                out[b, i >> 1, p, i & 1] = tiles[i]


def second_kernel(state, angle, tans, table, out, held):
    block0, middle0 = tans[BLOCK], tans[MIDDLE]
    row1, block1, middle1 = tans[3 + ROW], tans[3 + BLOCK], tans[3 + MIDDLE]
    turned = jnp.broadcast_to(angle[1:2], (8, 128))

    @pl.loop(0, 32)
    def _(j):
        for p in range(2):
            tiles = rotate_all([state[i, j >> 1, p, j & 1] for i in range(8)], [middle0] * 3)
            for i in range(8):
                held[p, i, j] = tiles[i]

    @pl.loop(0, 8)
    def _(b):
        parts = [[None] * 32, [None] * 32]
        for r in range(2):
            two = []
            for p in range(2):
                tiles = [held[p, b, 2 * q + r] for q in range(16)]
                two.append(rotate_all(tiles, [middle0, block0, block0, block0]))
            for q in range(16):
                re, im = phase(two[0][q], two[1][q], state[b, q, 2, r], turned)
                parts[0][2 * q + r], parts[1][2 * q + r] = re, im
        for p in range(2):
            tiles = mix_lanes(parts[p], table)
            tiles = rotate_all(tiles, [middle1, block1, block1, block1, row1])
            tiles = rotate_sublanes(tiles, row1)
            for i in range(32):
                held[p, b, i] = tiles[i]

    @pl.loop(0, 32)
    def _(j):
        for p in range(2):
            tiles = rotate_all([held[p, i, j] for i in range(8)], [middle1] * 3)
            for i in range(8):
                out[i, j >> 1, p, j & 1] = tiles[i]


def third_kernel(state, tans, out_hbm, held, done, sems):
    row, block = tans[3 + ROW], tans[3 + BLOCK]

    @pl.loop(0, 32)
    def _(j):
        for p in range(2):
            tiles = rotate_all([state[i, j >> 1, p, j & 1] for i in range(8)], [block] * 3)
            for i in range(8):
                held[p, i, j] = tiles[i]

    copies = []
    for b in range(8):
        for p in range(2):
            for r in range(2):
                tiles = rotate_all([held[p, b, 2 * q + r] for q in range(16)], [block, row, row, row])
                for q in range(16):
                    done[p, b, 2 * q + r] = tiles[q]
        copies.append(pltpu.make_async_copy(done.at[:, b], out_hbm.at[:, b], sems.at[b]))
        copies[-1].start()
    for c in copies:
        c.wait()


def spec(space):
    return pl.BlockSpec(memory_space=space)


def call(kernel, name, shapes, ins, outs, inputs, scratch, flops, limit):
    return pl.pallas_call(
        kernel,
        out_shape=[jax.ShapeDtypeStruct(s, d) for s, d in shapes],
        in_specs=[spec(s) for s in ins],
        out_specs=[spec(s) for s in outs],
        scratch_shapes=list(scratch),
        name=name,
        cost_estimate=pl.CostEstimate(flops=flops, bytes_accessed=5 << 20, transcendentals=0),
        compiler_params=pltpu.CompilerParams(vmem_limit_bytes=limit << 20),
    )(*inputs)


def exchange(state, shape):
    flat = lax.all_to_all(state.reshape(128, -1, 128), ORDER, 0, 0, tiled=True)
    return flat.reshape(shape)


def body(amplitudes, energies, diagonal_angles, turn_angles):
    f32, bf16 = jnp.float32, jnp.bfloat16
    table = VMEM((256, 256), bf16)
    state, tans, next_table = call(
        first_kernel,
        "first",
        [(SENT, f32), ((6, 8, 128), f32), ((256, 256), bf16)],
        [pltpu.HBM] * 4,
        [VMEM] * 3,
        (turn_angles, diagonal_angles, amplitudes.reshape(HOME), energies.reshape(8, 16, 2, 8, 128)),
        [
            SMEM((2, 4), f32),
            VMEM((2, 128), f32),
            VMEM(HOME, f32),
            table,
            pltpu.SemaphoreType.DMA((2 + 2 * PIECES,)),
        ],
        20_000_000,
        16,
    )
    state = exchange(state, SENT)
    (state,) = call(
        second_kernel,
        "second",
        [(AWAY, f32)],
        [VMEM] * 4,
        [VMEM],
        (state, diagonal_angles, tans, next_table),
        [VMEM(HOME, f32)],
        20_000_000,
        16,
    )
    state = exchange(state, AWAY)
    (state,) = call(
        third_kernel,
        "third",
        [(HOME, f32)],
        [VMEM] * 2,
        [pltpu.HBM],
        (state, tans),
        [VMEM(HOME, f32), VMEM(HOME, f32), pltpu.SemaphoreType.DMA((8,))],
        10_000_000,
        16,
    )
    return state.reshape(amplitudes.shape)


def solution(mesh):
    torus = Mesh(mesh.devices.reshape(4, 2, 4, 4), AXES)
    in_specs = (P(None, AXES, None, None), P(AXES, None, None), P(), P())
    out_specs = P(None, AXES, None, None)
    return jax.shard_map(body, mesh=torus, in_specs=in_specs, out_specs=out_specs, check_vma=False)
```

time: 327 us -> 106 us (0.32)
  waiting for transfers between devices: 133 us -> 0 us
  starting transfers between devices: 28.4 us -> 0 us
  matrix products: 20 us -> 0 us
  local copies, waits for them, and re-layouts: 20.3 us -> 4.17 us
  Pallas kernels: 0 us -> 14.1 us
  blocking collectives: 101 us -> 87.8 us
  other arithmetic: 11.5 us -> 0 us
  between operations: 11.5 us -> 0.02 us
    all_to_all x5 -> x0, waiting for transfers between devices: 133 us -> none  [the longest x2 56 us: body(): lax.all_to_all(values, 'lane', split_axis=3, concat_axis=1, tiled=True)]
    all_to_all x5 -> x0, starting transfers between devices: 28.4 us -> none  [the longest x2 11.7 us: body(): lax.all_to_all(values, BANK, split_axis=2, concat_axis=1, tiled=True)]
    dot_general x8 -> x0, matrix products: 20 us -> none  [mix_dim(): jnp.tensordot(values, real_part, axes=([dim], [0]), precision=lax.Precisi...]
    pallas_call x0 -> x3, Pallas kernels: none -> 14.1 us  [call(): pl.pallas_call(kernel, out_shape=[jax.ShapeDtypeStruct(s, d) for s, d in...]
    all_to_all x5 -> x2, blocking collectives: 101 us -> 87.8 us  [exchange(): flat = lax.all_to_all(state.reshape(128, -1, 128), ORDER, 0, 0, tiled=True)]
    another operation x2 -> x0, other arithmetic: 11.3 us -> none  [phase_step(): jnp.stack([values[0] * jnp.cos(turn) + values[1] * jnp.sin(turn), values[...]
    reshape x6 -> x0, local copies, waits for them, and re-layouts: 8.02 us -> none  [the longest x2 3.93 us: in_order(): return jnp.moveaxis(tiles, 0, dim).reshape(lengths)]
    transpose x4 -> x0, local copies, waits for them, and re-layouts: 5.18 us -> none  [mix_dim(): return jnp.moveaxis(moved, -1, dim)]
  transfers between devices with their start and end apart: 5 -> 0, of which waited for: 5 -> 0; matrix products, arithmetic and copies ran while one was open for 0% -> 0% of each run, Pallas kernels for 0% -> 0%
where the time goes in v2:
time: 106 us
  blocking collectives  87.8 us (83%)
  Pallas kernels  14.1 us (13%)
  local copies, waits for them, and re-layouts  4.17 us (4%)
    all_to_all x2, blocking collectives, exchange(): flat = lax.all_to_all(state.reshape(128, -1, 128), ORDER, 0, 0, tiled=True)  87.8 us
    pallas_call x3, Pallas kernels, call(): pl.pallas_call(kernel, out_shape=[jax.ShapeDtypeStruct(s, d) for s, d in...  14.1 us
    unnamed x8, local copies, waits for them, and re-layouts  4.17 us

profile of v2, /device:TPU:1, one launch (start us, length us, event | category | flops | bytes accessed | tf_op | source)
XLA Modules:
  0.0 106.2 jit_solution(2333018476837013871)
XLA Ops:
  0.0 0.0 copy-start
  0.0 1.6 %copy-done = f32[2,16,128,128]{3,2,1,0:T(8,128)S(1)} copy-done((f32[2,16,128,128]{3,2,1,0:T(8,128)S(1)}, f32[2,16,128,128]{3,2,1,0:T(8,128)}, u32[]{:S(2)}) %copy-start) | copy-done | bytes 2097176
  1.6 0.0 copy-start.1
  1.6 1.2 %copy-done.1 = f32[16,128,128]{2,1,0:T(8,128)S(1)} copy-done((f32[16,128,128]{2,1,0:T(8,128)S(1)}, f32[16,128,128]{2,1,0:T(8,128)}, u32[]{:S(2)}) %copy-start.1) | copy-done | bytes 1048600
  2.8 0.0 copy-start.2
  2.8 0.7 copy-done.2
  3.5 0.0 copy-start.3
  3.5 0.7 copy-done.3
  4.2 5.8 %first.1 = (f32[8,16,3,2,8,128]{5,4,3,2,1,0:T(8,128)S(1)}, f32[6,8,128]{2,1,0:T(8,128)S(1)}, bf16[256,256]{1,0:T(8,128)(2,1)S(1)}) custom-call(f32[2,4]{1,0:T(2,128)S(1)} %copy-done.3, f32[2,128]{1,0:T(2,128)S(1)} %copy-done.2, f32[2,8,32,8,128]{4,3,2,1,0:T(8,128)S(1)} %bitcast.11, f32[8,16,2,8,128]{4,3,2,1,0:T(8,128)S(1)} %bitcast.12), custom_call_target="tpu_custom_call" | custom-call | flops 20000000 | bytes 5242880 | tf_op jit(solution)/shard_map/first/pallas_call | solution.py:248
  10.0 52.9 %all_to_all.10 = f32[128,48,128]{2,1,0:T(8,128)S(1)} all-to-all(f32[128,48,128]{2,1,0:T(8,128)S(1)} %bitcast.10), channel_id=1, replica_groups=mesh['x'=4,'c'=2,'z'=4,'y'=4] {'y','z','x','c'}, dimensions={0} | all-to-all | bytes 6291456 | tf_op jit(solution)/shard_map/all_to_all | solution.py:261
  62.9 6.2 %second.1 = f32[8,16,2,2,8,128]{5,4,3,2,1,0:T(8,128)S(1)} custom-call(f32[8,16,3,2,8,128]{5,4,3,2,1,0:T(8,128)S(1)} %bitcast.7, f32[2,128]{1,0:T(2,128)S(1)} %copy-done.2, f32[6,8,128]{2,1,0:T(8,128)S(1)} %get-tuple-element.9.tans, bf16[256,256]{1,0:T(8,128)(2,1)S(1)} %get-tuple-element.10.table), custom_call_target="tpu_custom_call" | custom-call | flops 20000000 | bytes 5242880 | tf_op jit(solution)/shard_map/second/pallas_call | solution.py:248
  69.2 34.9 %all_to_all.11 = f32[128,32,128]{2,1,0:T(8,128)S(1)} all-to-all(f32[128,32,128]{2,1,0:T(8,128)S(1)} %bitcast.8), channel_id=1, replica_groups=mesh['x'=4,'c'=2,'z'=4,'y'=4] {'y','z','x','c'}, dimensions={0} | all-to-all | bytes 4194304 | tf_op jit(solution)/shard_map/all_to_all | solution.py:261
  104.1 2.1 %third.1 = f32[2,8,32,8,128]{4,3,2,1,0:T(8,128)} custom-call(f32[8,16,2,2,8,128]{5,4,3,2,1,0:T(8,128)S(1)} %bitcast.9, f32[6,8,128]{2,1,0:T(8,128)S(1)} %get-tuple-element.9.tans), custom_call_target="tpu_custom_call" | custom-call | flops 10000000 | bytes 5242880 | tf_op jit(solution)/shard_map/third/pallas_call | solution.py:248
Async XLA Ops:
  0.0 1.6 %copy-start = (f32[2,16,128,128]{3,2,1,0:T(8,128)S(1)}, f32[2,16,128,128]{3,2,1,0:T(8,128)}, u32[]{:S(2)}) copy-start(f32[2,16,128,128]{3,2,1,0:T(8,128)} %param.4) | copy-start | bytes 6291460
  1.6 1.2 %copy-start.1 = (f32[16,128,128]{2,1,0:T(8,128)S(1)}, f32[16,128,128]{2,1,0:T(8,128)}, u32[]{:S(2)}) copy-start(f32[16,128,128]{2,1,0:T(8,128)} %param.5) | copy-start | bytes 3145732
  2.8 0.7 copy-start.2
  3.5 0.7 copy-start.3

commit v3 on v2

--- a/solution.py
+++ b/solution.py
@@ -25,8 +25,8 @@
     return [float(c) for c in series.convert(kind=np.polynomial.Polynomial).coef]
 
 
-COS = fit(np.cos, 8)
-SIN = fit(lambda t: np.sinc(t / np.pi), 7)
+COS = fit(lambda t: np.sqrt(2) * np.cos(t / 2), 5)
+SIN = fit(lambda t: np.sqrt(0.5) * np.sinc(t / 2 / np.pi), 5)
 
 
 def horner(coef, s):
@@ -38,7 +38,8 @@
 
 def cos_sin(turn):
     square = turn * turn
-    return horner(COS, square), horner(SIN, square) * turn
+    cos, sin = horner(COS, square), horner(SIN, square) * turn
+    return 1.0 - sin * sin, sin * cos
 
 
 def phase(re, im, level, angle):
@@ -67,15 +68,8 @@
     place = lax.broadcasted_iota(jnp.int32, (8, 128), 0)
     for bit in range(3):
         step = 1 << bit
-        one = (place & step) != 0
-        weight = jnp.where(one, tan, -tan)
-        out = []
-        for t in tiles:
-            other = pltpu.roll(t, step, 0)
-            if step < 4:
-                other = jnp.where(one, other, pltpu.roll(t, 8 - step, 0))
-            out.append(t + weight * other)
-        tiles = out
+        weight = jnp.where((place & step) != 0, tan, -tan)
+        tiles = [t + weight * jnp.take_along_axis(t, place ^ step, axis=0) for t in tiles]
     return tiles
 
 
@@ -271,7 +265,15 @@
         [(SENT, f32), ((6, 8, 128), f32), ((256, 256), bf16)],
         [pltpu.HBM] * 4,
         [VMEM] * 3,
-        (turn_angles, diagonal_angles, amplitudes.reshape(HOME), energies.reshape(8, 16, 2, 8, 128)),
+        [
+            pltpu.with_memory_space_constraint(a, pltpu.HBM)
+            for a in (
+                turn_angles,
+                diagonal_angles,
+                amplitudes.reshape(HOME),
+                energies.reshape(8, 16, 2, 8, 128),
+            )
+        ],
         [
             SMEM((2, 4), f32),
             VMEM((2, 128), f32),

time: 106 us -> 102 us (0.962)
  local copies, waits for them, and re-layouts: 4.17 us -> 0.01 us
    unnamed x8 -> x2, local copies, waits for them, and re-layouts: 4.17 us -> 0.01 us
where the time goes in v3:
time: 102 us
  blocking collectives  87.8 us (86%)
  Pallas kernels  13.7 us (13%)
    all_to_all x2, blocking collectives, exchange(): flat = lax.all_to_all(state.reshape(128, -1, 128), ORDER, 0, 0, tiled=True)  87.8 us
    pallas_call x3, Pallas kernels, call(): pl.pallas_call(kernel, out_shape=[jax.ShapeDtypeStruct(s, d) for s, d in...  13.7 us

profile of v3, /device:TPU:1, one launch (start us, length us, event | category | flops | bytes accessed | tf_op | source)
XLA Modules:
  0.0 101.5 jit_solution(3003414344310989724)
XLA Ops:
  0.0 5.9 %first.1 = (f32[8,16,3,2,8,128]{5,4,3,2,1,0:T(8,128)S(1)}, f32[6,8,128]{2,1,0:T(8,128)S(1)}, bf16[256,256]{1,0:T(8,128)(2,1)S(1)}) custom-call(f32[2,4]{1,0:T(2,128)} %turn_hbm.1, f32[2,128]{1,0:T(2,128)} %angle.1, f32[2,8,32,8,128]{4,3,2,1,0:T(8,128)} %bitcast.11, f32[8,16,2,8,128]{4,3,2,1,0:T(8,128)} %bitcast.12), custom_call_target="tpu_custom_call" | custom-call | flops 20000000 | bytes 5242880 | tf_op jit(solution)/shard_map/first/pallas_call | solution.py:242
  5.9 0.0 copy-start
  5.9 52.9 %all_to_all.10 = f32[128,48,128]{2,1,0:T(8,128)S(1)} all-to-all(f32[128,48,128]{2,1,0:T(8,128)S(1)} %bitcast.10), channel_id=1, replica_groups=mesh['x'=4,'c'=2,'z'=4,'y'=4] {'y','z','x','c'}, dimensions={0} | all-to-all | bytes 6291456 | tf_op jit(solution)/shard_map/all_to_all | solution.py:255
  58.8 0.0 copy-done
  58.8 5.7 %second.1 = f32[8,16,2,2,8,128]{5,4,3,2,1,0:T(8,128)S(1)} custom-call(f32[8,16,3,2,8,128]{5,4,3,2,1,0:T(8,128)S(1)} %bitcast.7, f32[2,128]{1,0:T(2,128)S(1)} %copy-done, f32[6,8,128]{2,1,0:T(8,128)S(1)} %get-tuple-element.9.tans, bf16[256,256]{1,0:T(8,128)(2,1)S(1)} %get-tuple-element.10.table), custom_call_target="tpu_custom_call" | custom-call | flops 20000000 | bytes 5242880 | tf_op jit(solution)/shard_map/second/pallas_call | solution.py:242
  64.5 34.9 %all_to_all.11 = f32[128,32,128]{2,1,0:T(8,128)S(1)} all-to-all(f32[128,32,128]{2,1,0:T(8,128)S(1)} %bitcast.8), channel_id=1, replica_groups=mesh['x'=4,'c'=2,'z'=4,'y'=4] {'y','z','x','c'}, dimensions={0} | all-to-all | bytes 4194304 | tf_op jit(solution)/shard_map/all_to_all | solution.py:255
  99.5 2.1 %third.1 = f32[2,8,32,8,128]{4,3,2,1,0:T(8,128)} custom-call(f32[8,16,2,2,8,128]{5,4,3,2,1,0:T(8,128)S(1)} %bitcast.9, f32[6,8,128]{2,1,0:T(8,128)S(1)} %get-tuple-element.9.tans), custom_call_target="tpu_custom_call" | custom-call | flops 10000000 | bytes 5242880 | tf_op jit(solution)/shard_map/third/pallas_call | solution.py:242
Async XLA Ops:
  5.9 52.9 %copy-start = (f32[2,128]{1,0:T(2,128)S(1)}, f32[2,128]{1,0:T(2,128)}, u32[]{:S(2)}) copy-start(f32[2,128]{1,0:T(2,128)} %angle.1) | copy-start | bytes 3076

commit v4 on v3

v4 whole, which is shorter than its diff:
```python
import jax
import jax.numpy as jnp
import numpy as np
from jax import lax
from jax.experimental import pallas as pl
from jax.experimental.pallas import tpu as pltpu
from jax.sharding import Mesh
from jax.sharding import PartitionSpec as P

AXES = ("x", "c", "z", "y")
ORDER = ("y", "z", "x", "c")
VMEM = pltpu.VMEM
SMEM = pltpu.SMEM
AHEAD = 4
HOME = (2, 8, 32, 8, 128)
SENT = (8, 16, 3, 2, 8, 128)
AWAY = (8, 16, 2, 2, 8, 128)
LANES, ROWS, BLOCK, MIDDLE = range(4)


def fit(fn, terms, most=5.77):
    k = np.arange(400)
    s = most / 2 * (1 + np.cos(np.pi * (k + 0.5) / 400))
    series = np.polynomial.Chebyshev.fit(s, fn(np.sqrt(s)), terms - 1, domain=[0, most])
    return [float(c) for c in series.convert(kind=np.polynomial.Polynomial).coef]


COS = fit(lambda t: np.sqrt(2) * np.cos(t / 2), 5)
SIN = fit(lambda t: np.sqrt(0.5) * np.sinc(t / 2 / np.pi), 5)


def horner(coef, s):
    total = s * coef[-1] + coef[-2]
    for c in coef[-3::-1]:
        total = total * s + c
    return total


def cos_sin(turn):
    square = turn * turn
    cos, sin = horner(COS, square), horner(SIN, square) * turn
    return 1.0 - sin * sin, sin * cos


def phase(re, im, level, angle):
    cos, sin = cos_sin(level * angle)
    return re * cos + im * sin, im * cos - re * sin


def rotate(tiles, bit, tan):
    step = 1 << bit
    out = list(tiles)
    for i, u in enumerate(tiles):
        if not i & step:
            v = tiles[i + step]
            out[i] = u - tan * v
            out[i + step] = v + tan * u
    return out


def rotate_all(tiles, tans):
    for bit, tan in zip(reversed(range(len(tans))), tans):
        tiles = rotate(tiles, bit, tan)
    return tiles


def kron(columns, pairs):
    tiles = [columns]
    for zero, one in pairs:
        tiles = [t * f for t in tiles for f in (zero, one)]
    return tiles


def split(values):
    high = values.astype(jnp.bfloat16)
    return high, (values - high.astype(jnp.float32)).astype(jnp.bfloat16)


def turn_factors(turn, layer):
    pairs = [cos_sin(jnp.full((8, 128), turn[layer, g], jnp.float32)) for g in range(4)]
    return [c for c, _ in pairs], [s for _, s in pairs]


def store_tables(cos, sin, rest, bits, lanes_ref, rows_ref):
    col = lax.broadcasted_iota(jnp.int32, (8, 128), 1)
    sub = lax.broadcasted_iota(jnp.int32, (8, 128), 0)

    def pair(bit, cos, sin, back):
        one = ((col >> bit) & 1) == 1
        if back:
            return jnp.where(one, -sin, cos), jnp.where(one, cos, sin)
        return jnp.where(one, sin, cos), jnp.where(one, cos, -sin)

    def low(cos, sin, back):
        table = jnp.ones((8, 128), jnp.float32)
        for bit in range(3):
            zero, one = pair(bit, cos, sin, back)
            table = table * jnp.where(((sub >> bit) & 1) == 1, one, zero)
        return table

    tiles = kron(low(cos[0], sin[0], False) * rest, [pair(k, cos[0], sin[0], False) for k in (6, 5, 4, 3)])
    for k, t in enumerate(tiles):
        high, less = split(t)
        rows, more = slice(8 * k, 8 * k + 8), slice(128 + 8 * k, 136 + 8 * k)
        lanes_ref[rows, 0:128] = high
        lanes_ref[rows, 128:256] = less
        lanes_ref[more, 0:128] = high
        lanes_ref[more, 128:256] = jnp.zeros_like(high)
    tiles = low(cos[ROWS], sin[ROWS], True)
    g = bits[0]
    for half, top in enumerate(((cos[g], sin[g]), (-sin[g], cos[g]))):
        pairs = [pair(6 - k, cos[h], sin[h], True) for k, h in enumerate(bits[1:])]
        for k, t in enumerate(kron(tiles, [top] + pairs)):
            high, less = split(t)
            rows = slice(8 * k, 8 * k + 8)
            for third, part in enumerate((high, high, less)):
                at = 256 * third + 128 * half
                rows_ref[rows, at : at + 128] = part


def mix(parts, lanes_ref, rows_ref):
    highs, lows = [], []
    for tiles in parts:
        both = jnp.dot(
            jnp.concatenate(split(jnp.concatenate(tiles, axis=0)), axis=1),
            lanes_ref[...],
            preferred_element_type=jnp.float32,
        )
        high, low = split(both[:, 0:128] + both[:, 128:256])
        highs.append(high)
        lows.append(low)
    high, low = jnp.concatenate(highs, axis=1), jnp.concatenate(lows, axis=1)
    mixed = jnp.dot(
        rows_ref[...], jnp.concatenate([high, low, high], axis=0), preferred_element_type=jnp.float32
    )
    return [[mixed[8 * i : 8 * i + 8, 128 * p : 128 * p + 128] for i in range(32)] for p in range(2)]


def in_step(prepare, finish, blocks):
    for k in range(5):
        now, last = blocks[k % 2], blocks[(k + 1) % 2]
        if k < 4:
            prepare(2 * k, now, 0)
            prepare(2 * k + 1, now, 1)
        if k:
            finish(2 * k - 2, last, 0)
            finish(2 * k - 1, last, 1)


def mix_block(block, at, lanes, rows, held, b):
    parts = mix([[block[at, p, i] for i in range(32)] for p in range(2)], lanes, rows)
    for p in range(2):
        for i in range(32):
            held[p, b, i] = parts[p][i]


def first_kernel(
    turn_hbm,
    angle_hbm,
    state_hbm,
    levels_hbm,
    out,
    tans,
    next_lanes,
    next_rows,
    turn,
    angle,
    state,
    lanes,
    rows,
    even,
    odd,
    sems,
):
    small = [
        pltpu.make_async_copy(turn_hbm, turn, sems.at[0]),
        pltpu.make_async_copy(angle_hbm, angle, sems.at[1]),
    ]
    copies = [
        (
            pltpu.make_async_copy(levels_hbm.at[b], out.at[b, :, 2], sems.at[2 + 2 * b]),
            pltpu.make_async_copy(state_hbm.at[:, b], state.at[:, b], sems.at[3 + 2 * b]),
        )
        for b in range(8)
    ]

    def start(b):
        for c in copies[b]:
            c.start()

    for c in small:
        c.start()
    for b in range(AHEAD):
        start(b)
    for c in small:
        c.wait()
    cos, sin = turn_factors(turn, 0)
    for g in range(1, 4):
        tans[g] = sin[g] / cos[g]
    block0 = tans[BLOCK]
    two, four = cos[BLOCK] * cos[BLOCK], cos[MIDDLE] * cos[MIDDLE]
    rest = two * two * two * four * four
    store_tables(cos, sin, rest, (BLOCK, ROWS, ROWS, ROWS, ROWS), lanes, rows)
    cos, sin = turn_factors(turn, 1)
    for g in range(1, 4):
        tans[4 + g] = sin[g] / cos[g]
    pair = cos[ROWS] * cos[BLOCK] * cos[MIDDLE]
    rest = pair * pair * pair * cos[BLOCK]
    store_tables(cos, sin, rest, (MIDDLE, BLOCK, BLOCK, BLOCK, ROWS), next_lanes, next_rows)
    turned = jnp.broadcast_to(angle[0:1], (8, 128))

    def prepare(b, block, at):
        if not at:
            for k in (b, b + 1):
                for c in copies[k]:
                    c.wait()
                if k + AHEAD < 8:
                    start(k + AHEAD)
        for i in range(32):
            level = out[b, i >> 1, 2, i & 1]
            block[at, 0, i], block[at, 1, i] = phase(state[0, b, i], state[1, b, i], level, turned)

    def finish(b, block, at):
        mix_block(block, at, lanes, rows, state, b)

    in_step(prepare, finish, (even, odd))

    @pl.loop(0, 32, unroll=4)
    def _(j):
        for p in range(2):
            tiles = rotate_all([state[p, i, j] for i in range(8)], [block0] * 3)
            for i in range(8):
                out[i, j >> 1, p, j & 1] = tiles[i]


def second_kernel(state, angle, tans, lanes, rows, out, held, even, odd):
    block0, middle0, middle1 = tans[BLOCK], tans[MIDDLE], tans[4 + MIDDLE]
    turned = jnp.broadcast_to(angle[1:2], (8, 128))

    @pl.loop(0, 32, unroll=4)
    def _(j):
        for p in range(2):
            tiles = rotate_all([state[i, j >> 1, p, j & 1] for i in range(8)], [middle0] * 3)
            for i in range(8):
                held[p, i, j] = tiles[i]

    def prepare(b, block, at):
        for r in range(2):
            re, im = (
                rotate_all([held[p, b, 2 * q + r] for q in range(16)], [middle0, block0, block0, block0])
                for p in range(2)
            )
            for q in range(16):
                level = state[b, q, 2, r]
                i = 2 * q + r
                block[at, 0, i], block[at, 1, i] = phase(re[q], im[q], level, turned)

    def finish(b, block, at):
        mix_block(block, at, lanes, rows, held, b)

    in_step(prepare, finish, (even, odd))

    @pl.loop(0, 32, unroll=4)
    def _(j):
        for p in range(2):
            tiles = rotate_all([held[p, i, j] for i in range(8)], [middle1] * 3)
            for i in range(8):
                out[i, j >> 1, p, j & 1] = tiles[i]


def third_kernel(state, tans, out_hbm, held, done, sems):
    row, block = tans[4 + ROWS], tans[4 + BLOCK]

    @pl.loop(0, 32, unroll=4)
    def _(j):
        for p in range(2):
            tiles = rotate_all([state[i, j >> 1, p, j & 1] for i in range(8)], [block] * 3)
            for i in range(8):
                held[p, i, j] = tiles[i]

    copies = []
    for b in range(8):
        for p in range(2):
            for r in range(2):
                tiles = rotate_all([held[p, b, 2 * q + r] for q in range(16)], [block, row, row, row])
                for q in range(16):
                    done[p, b, 2 * q + r] = tiles[q]
        copies.append(pltpu.make_async_copy(done.at[:, b], out_hbm.at[:, b], sems.at[b]))
        copies[-1].start()
    for c in copies:
        c.wait()


def spec(space):
    return pl.BlockSpec(memory_space=space)


def call(kernel, name, shapes, ins, outs, inputs, scratch, flops, limit):
    return pl.pallas_call(
        kernel,
        out_shape=[jax.ShapeDtypeStruct(s, d) for s, d in shapes],
        in_specs=[spec(s) for s in ins],
        out_specs=[spec(s) for s in outs],
        scratch_shapes=list(scratch),
        name=name,
        cost_estimate=pl.CostEstimate(flops=flops, bytes_accessed=5 << 20, transcendentals=0),
        compiler_params=pltpu.CompilerParams(vmem_limit_bytes=limit << 20),
    )(*inputs)


def exchange(state, shape):
    flat = lax.all_to_all(state.reshape(128, -1, 128), ORDER, 0, 0, tiled=True)
    return flat.reshape(shape)


def body(amplitudes, energies, diagonal_angles, turn_angles):
    f32, bf16 = jnp.float32, jnp.bfloat16
    block = VMEM((2, 2, 32, 8, 128), f32)
    state, tans, lanes, rows = call(
        first_kernel,
        "first",
        [(SENT, f32), ((8, 8, 128), f32), ((256, 256), bf16), ((256, 768), bf16)],
        [pltpu.HBM] * 4,
        [VMEM] * 4,
        [
            pltpu.with_memory_space_constraint(a, pltpu.HBM)
            for a in (
                turn_angles,
                diagonal_angles,
                amplitudes.reshape(HOME),
                energies.reshape(8, 16, 2, 8, 128),
            )
        ],
        [
            SMEM((2, 4), f32),
            VMEM((2, 128), f32),
            VMEM(HOME, f32),
            VMEM((256, 256), bf16),
            VMEM((256, 768), bf16),
            block,
            block,
            pltpu.SemaphoreType.DMA((18,)),
        ],
        20_000_000,
        16,
    )
    state = exchange(state, SENT)
    (state,) = call(
        second_kernel,
        "second",
        [(AWAY, f32)],
        [VMEM] * 5,
        [VMEM],
        (state, diagonal_angles, tans, lanes, rows),
        [VMEM(HOME, f32), block, block],
        20_000_000,
        16,
    )
    state = exchange(state, AWAY)
    (state,) = call(
        third_kernel,
        "third",
        [(HOME, f32)],
        [VMEM] * 2,
        [pltpu.HBM],
        (state, tans),
        [VMEM(HOME, f32), VMEM(HOME, f32), pltpu.SemaphoreType.DMA((8,))],
        10_000_000,
        16,
    )
    return state.reshape(amplitudes.shape)


def solution(mesh):
    torus = Mesh(mesh.devices.reshape(4, 2, 4, 4), AXES)
    in_specs = (P(None, AXES, None, None), P(AXES, None, None), P(), P())
    out_specs = P(None, AXES, None, None)
    return jax.shard_map(body, mesh=torus, in_specs=in_specs, out_specs=out_specs, check_vma=False)
```

time: 102 us -> 99.1 us (0.972)
  Pallas kernels: 13.7 us -> 11.1 us
    pallas_call x3, Pallas kernels: 13.7 us -> 11.1 us  [call(): pl.pallas_call(kernel, out_shape=[jax.ShapeDtypeStruct(s, d) for s, d in...]
where the time goes in v4:
time: 99.1 us; the launch traced here: 99 us
  blocking collectives  87.8 us (89%)
  Pallas kernels  11.1 us (11%)
    all_to_all x2, blocking collectives, exchange(): flat = lax.all_to_all(state.reshape(128, -1, 128), ORDER, 0, 0, tiled=True)  87.8 us
    pallas_call x3, Pallas kernels, call(): pl.pallas_call(kernel, out_shape=[jax.ShapeDtypeStruct(s, d) for s, d in...  11.1 us

profile of v4, /device:TPU:1, one launch (start us, length us, event | category | flops | bytes accessed | tf_op | source)
XLA Modules:
  0.0 99.0 jit_solution(10011708748905446942)
XLA Ops:
  0.0 5.0 %first.1 = (f32[8,16,3,2,8,128]{5,4,3,2,1,0:T(8,128)S(1)}, f32[8,8,128]{2,1,0:T(8,128)S(1)}, bf16[256,256]{1,0:T(8,128)(2,1)S(1)}, bf16[256,768]{1,0:T(8,128)(2,1)S(1)}) custom-call(f32[2,4]{1,0:T(2,128)} %turn_hbm.1, f32[2,128]{1,0:T(2,128)} %angle.1, f32[2,8,32,8,128]{4,3,2,1,0:T(8,128)} %bitcast.11, f32[8,16,2,8,128]{4,3,2,1,0:T(8,128)} %bitcast.12), custom_call_target="tpu_custom_call" | custom-call | flops 20000000 | bytes 5242880 | tf_op jit(solution)/shard_map/first/pallas_call | solution.py:299
  5.0 0.0 copy-start
  5.0 52.9 %all_to_all.10 = f32[128,48,128]{2,1,0:T(8,128)S(1)} all-to-all(f32[128,48,128]{2,1,0:T(8,128)S(1)} %bitcast.10), channel_id=1, replica_groups=mesh['x'=4,'c'=2,'z'=4,'y'=4] {'y','z','x','c'}, dimensions={0} | all-to-all | bytes 6291456 | tf_op jit(solution)/shard_map/all_to_all | solution.py:312
  57.9 0.0 copy-done
  57.9 4.2 %second.1 = f32[8,16,2,2,8,128]{5,4,3,2,1,0:T(8,128)S(1)} custom-call(f32[8,16,3,2,8,128]{5,4,3,2,1,0:T(8,128)S(1)} %bitcast.7, f32[2,128]{1,0:T(2,128)S(1)} %copy-done, f32[8,8,128]{2,1,0:T(8,128)S(1)} %get-tuple-element.10.tans, bf16[256,256]{1,0:T(8,128)(2,1)S(1)} %get-tuple-element.11.lanes, bf16[256,768]{1,0:T(8,128)(2,1)S(1)} %get-tuple-element.12.rows), custom_call_target="tpu_custom_call" | custom-call | flops 20000000 | bytes 5242880 | tf_op jit(solution)/shard_map/second/pallas_call | solution.py:299
  62.1 34.9 %all_to_all.11 = f32[128,32,128]{2,1,0:T(8,128)S(1)} all-to-all(f32[128,32,128]{2,1,0:T(8,128)S(1)} %bitcast.8), channel_id=1, replica_groups=mesh['x'=4,'c'=2,'z'=4,'y'=4] {'y','z','x','c'}, dimensions={0} | all-to-all | bytes 4194304 | tf_op jit(solution)/shard_map/all_to_all | solution.py:312
  97.0 1.9 %third.1 = f32[2,8,32,8,128]{4,3,2,1,0:T(8,128)} custom-call(f32[8,16,2,2,8,128]{5,4,3,2,1,0:T(8,128)S(1)} %bitcast.9, f32[8,8,128]{2,1,0:T(8,128)S(1)} %get-tuple-element.10.tans), custom_call_target="tpu_custom_call" | custom-call | flops 10000000 | bytes 5242880 | tf_op jit(solution)/shard_map/third/pallas_call | solution.py:299
Async XLA Ops:
  5.0 52.9 %copy-start = (f32[2,128]{1,0:T(2,128)S(1)}, f32[2,128]{1,0:T(2,128)}, u32[]{:S(2)}) copy-start(f32[2,128]{1,0:T(2,128)} %angle.1) | copy-start | bytes 3076

commit v5 on v4

--- a/solution.py
+++ b/solution.py
@@ -11,7 +11,6 @@
 ORDER = ("y", "z", "x", "c")
 VMEM = pltpu.VMEM
 SMEM = pltpu.SMEM
-AHEAD = 4
 HOME = (2, 8, 32, 8, 128)
 SENT = (8, 16, 3, 2, 8, 128)
 AWAY = (8, 16, 2, 2, 8, 128)
@@ -25,8 +24,7 @@
     return [float(c) for c in series.convert(kind=np.polynomial.Polynomial).coef]
 
 
-COS = fit(lambda t: np.sqrt(2) * np.cos(t / 2), 5)
-SIN = fit(lambda t: np.sqrt(0.5) * np.sinc(t / 2 / np.pi), 5)
+SIN = fit(lambda t: np.sqrt(0.5) * np.sinc(t / 2 / np.pi), 4)
 
 
 def horner(coef, s):
@@ -37,9 +35,10 @@
 
 
 def cos_sin(turn):
-    square = turn * turn
-    cos, sin = horner(COS, square), horner(SIN, square) * turn
-    return 1.0 - sin * sin, sin * cos
+    half = horner(SIN, turn * turn) * turn
+    cos = 1.0 - half * half
+    above = 1.0 + cos
+    return cos, half * above * lax.rsqrt(above)
 
 
 def phase(re, im, level, angle):
@@ -119,21 +118,19 @@
 
 
 def mix(parts, lanes_ref, rows_ref):
-    highs, lows = [], []
-    for tiles in parts:
-        both = jnp.dot(
-            jnp.concatenate(split(jnp.concatenate(tiles, axis=0)), axis=1),
-            lanes_ref[...],
-            preferred_element_type=jnp.float32,
+    rows = jnp.concatenate([t for tiles in parts for t in tiles], axis=0)
+    both = jnp.dot(
+        jnp.concatenate(split(rows), axis=1), lanes_ref[...], preferred_element_type=jnp.float32
+    )
+    high, low = split(both[:, 0:128] + both[:, 128:256])
+    out = []
+    for b in range(0, 256 * len(parts), 512):
+        h, l = (jnp.concatenate([v[b : b + 256], v[b + 256 : b + 512]], axis=1) for v in (high, low))
+        mixed = jnp.dot(
+            rows_ref[...], jnp.concatenate([h, l, h], axis=0), preferred_element_type=jnp.float32
         )
-        high, low = split(both[:, 0:128] + both[:, 128:256])
-        highs.append(high)
-        lows.append(low)
-    high, low = jnp.concatenate(highs, axis=1), jnp.concatenate(lows, axis=1)
-    mixed = jnp.dot(
-        rows_ref[...], jnp.concatenate([high, low, high], axis=0), preferred_element_type=jnp.float32
-    )
-    return [[mixed[8 * i : 8 * i + 8, 128 * p : 128 * p + 128] for i in range(32)] for p in range(2)]
+        out += [[mixed[8 * i : 8 * i + 8, 128 * p : 128 * p + 128] for i in range(32)] for p in range(2)]
+    return out
 
 
 def in_step(prepare, finish, blocks):
@@ -143,15 +140,16 @@
             prepare(2 * k, now, 0)
             prepare(2 * k + 1, now, 1)
         if k:
-            finish(2 * k - 2, last, 0)
-            finish(2 * k - 1, last, 1)
-
-
-def mix_block(block, at, lanes, rows, held, b):
-    parts = mix([[block[at, p, i] for i in range(32)] for p in range(2)], lanes, rows)
-    for p in range(2):
+            finish(2 * k - 2, last)
+
+
+def mix_blocks(block, lanes, rows, held, b):
+    parts = mix(
+        [[block[at, p, i] for i in range(32)] for at in range(2) for p in range(2)], lanes, rows
+    )
+    for k, tiles in enumerate(parts):
         for i in range(32):
-            held[p, b, i] = parts[p][i]
+            held[k % 2, b + k // 2, i] = tiles[i]
 
 
 def first_kernel(
@@ -184,14 +182,11 @@
         for b in range(8)
     ]
 
-    def start(b):
-        for c in copies[b]:
-            c.start()
-
     for c in small:
         c.start()
-    for b in range(AHEAD):
-        start(b)
+    for pair in copies:
+        for c in pair:
+            c.start()
     for c in small:
         c.wait()
     cos, sin = turn_factors(turn, 0)
@@ -201,27 +196,29 @@
     two, four = cos[BLOCK] * cos[BLOCK], cos[MIDDLE] * cos[MIDDLE]
     rest = two * two * two * four * four
     store_tables(cos, sin, rest, (BLOCK, ROWS, ROWS, ROWS, ROWS), lanes, rows)
-    cos, sin = turn_factors(turn, 1)
-    for g in range(1, 4):
-        tans[4 + g] = sin[g] / cos[g]
-    pair = cos[ROWS] * cos[BLOCK] * cos[MIDDLE]
-    rest = pair * pair * pair * cos[BLOCK]
-    store_tables(cos, sin, rest, (MIDDLE, BLOCK, BLOCK, BLOCK, ROWS), next_lanes, next_rows)
     turned = jnp.broadcast_to(angle[0:1], (8, 128))
+
+    def later_tables():
+        cos, sin = turn_factors(turn, 1)
+        for g in range(1, 4):
+            tans[4 + g] = sin[g] / cos[g]
+        pair = cos[ROWS] * cos[BLOCK] * cos[MIDDLE]
+        rest = pair * pair * pair * cos[BLOCK]
+        store_tables(cos, sin, rest, (MIDDLE, BLOCK, BLOCK, BLOCK, ROWS), next_lanes, next_rows)
 
     def prepare(b, block, at):
         if not at:
-            for k in (b, b + 1):
-                for c in copies[k]:
+            for pair in copies[b : b + 2] if b < 2 else copies[2:] if b == 2 else ():
+                for c in pair:
                     c.wait()
-                if k + AHEAD < 8:
-                    start(k + AHEAD)
+            if b == 4:
+                later_tables()
         for i in range(32):
             level = out[b, i >> 1, 2, i & 1]
             block[at, 0, i], block[at, 1, i] = phase(state[0, b, i], state[1, b, i], level, turned)
 
-    def finish(b, block, at):
-        mix_block(block, at, lanes, rows, state, b)
+    def finish(b, block):
+        mix_blocks(block, lanes, rows, state, b)
 
     in_step(prepare, finish, (even, odd))
 
@@ -255,8 +252,8 @@
                 i = 2 * q + r
                 block[at, 0, i], block[at, 1, i] = phase(re[q], im[q], level, turned)
 
-    def finish(b, block, at):
-        mix_block(block, at, lanes, rows, held, b)
+    def finish(b, block):
+        mix_blocks(block, lanes, rows, held, b)
 
     in_step(prepare, finish, (even, odd))
 
@@ -270,23 +267,22 @@
 
 def third_kernel(state, tans, out_hbm, held, done, sems):
     row, block = tans[4 + ROWS], tans[4 + BLOCK]
-
-    @pl.loop(0, 32, unroll=4)
-    def _(j):
-        for p in range(2):
+    copies = []
+    for p in range(2):
+
+        @pl.loop(0, 32, unroll=4)
+        def _(j):
             tiles = rotate_all([state[i, j >> 1, p, j & 1] for i in range(8)], [block] * 3)
             for i in range(8):
                 held[p, i, j] = tiles[i]
 
-    copies = []
-    for b in range(8):
-        for p in range(2):
+        for b in range(8):
             for r in range(2):
                 tiles = rotate_all([held[p, b, 2 * q + r] for q in range(16)], [block, row, row, row])
                 for q in range(16):
                     done[p, b, 2 * q + r] = tiles[q]
-        copies.append(pltpu.make_async_copy(done.at[:, b], out_hbm.at[:, b], sems.at[b]))
-        copies[-1].start()
+            copies.append(pltpu.make_async_copy(done.at[p, b], out_hbm.at[p, b], sems.at[8 * p + b]))
+            copies[-1].start()
     for c in copies:
         c.wait()
 
@@ -364,7 +360,7 @@
         [VMEM] * 2,
         [pltpu.HBM],
         (state, tans),
-        [VMEM(HOME, f32), VMEM(HOME, f32), pltpu.SemaphoreType.DMA((8,))],
+        [VMEM(HOME, f32), VMEM(HOME, f32), pltpu.SemaphoreType.DMA((16,))],
         10_000_000,
         16,
     )

time: 99.1 us -> 98.2 us (level)
  no operation moved by 1% of the time
where the time goes in v5:
time: 98.2 us; the launch traced here: 98.1 us
  blocking collectives  87.8 us (89%)
  Pallas kernels  10.2 us (10%)
    all_to_all x2, blocking collectives, exchange(): flat = lax.all_to_all(state.reshape(128, -1, 128), ORDER, 0, 0, tiled=True)  87.8 us
    pallas_call x3, Pallas kernels, call(): pl.pallas_call(kernel, out_shape=[jax.ShapeDtypeStruct(s, d) for s, d in...  10.2 us

profile of v5, /device:TPU:1, one launch (start us, length us, event | category | flops | bytes accessed | tf_op | source)
XLA Modules:
  0.0 98.1 jit_solution(4750824925787864336)
XLA Ops:
  0.0 4.6 %first.1 = (f32[8,16,3,2,8,128]{5,4,3,2,1,0:T(8,128)S(1)}, f32[8,8,128]{2,1,0:T(8,128)S(1)}, bf16[256,256]{1,0:T(8,128)(2,1)S(1)}, bf16[256,768]{1,0:T(8,128)(2,1)S(1)}) custom-call(f32[2,4]{1,0:T(2,128)} %turn_hbm.1, f32[2,128]{1,0:T(2,128)} %angle.1, f32[2,8,32,8,128]{4,3,2,1,0:T(8,128)} %bitcast.11, f32[8,16,2,8,128]{4,3,2,1,0:T(8,128)} %bitcast.12), custom_call_target="tpu_custom_call" | custom-call | flops 20000000 | bytes 5242880 | tf_op jit(solution)/shard_map/first/pallas_call | solution.py:295
  4.7 0.0 copy-start
  4.7 52.9 %all_to_all.10 = f32[128,48,128]{2,1,0:T(8,128)S(1)} all-to-all(f32[128,48,128]{2,1,0:T(8,128)S(1)} %bitcast.10), channel_id=1, replica_groups=mesh['x'=4,'c'=2,'z'=4,'y'=4] {'y','z','x','c'}, dimensions={0} | all-to-all | bytes 6291456 | tf_op jit(solution)/shard_map/all_to_all | solution.py:308
  57.6 0.0 copy-done
  57.6 3.6 %second.1 = f32[8,16,2,2,8,128]{5,4,3,2,1,0:T(8,128)S(1)} custom-call(f32[8,16,3,2,8,128]{5,4,3,2,1,0:T(8,128)S(1)} %bitcast.7, f32[2,128]{1,0:T(2,128)S(1)} %copy-done, f32[8,8,128]{2,1,0:T(8,128)S(1)} %get-tuple-element.10.tans, bf16[256,256]{1,0:T(8,128)(2,1)S(1)} %get-tuple-element.11.lanes, bf16[256,768]{1,0:T(8,128)(2,1)S(1)} %get-tuple-element.12.rows), custom_call_target="tpu_custom_call" | custom-call | flops 20000000 | bytes 5242880 | tf_op jit(solution)/shard_map/second/pallas_call | solution.py:295
  61.2 34.9 %all_to_all.11 = f32[128,32,128]{2,1,0:T(8,128)S(1)} all-to-all(f32[128,32,128]{2,1,0:T(8,128)S(1)} %bitcast.8), channel_id=1, replica_groups=mesh['x'=4,'c'=2,'z'=4,'y'=4] {'y','z','x','c'}, dimensions={0} | all-to-all | bytes 4194304 | tf_op jit(solution)/shard_map/all_to_all | solution.py:308
  96.1 2.0 %third.1 = f32[2,8,32,8,128]{4,3,2,1,0:T(8,128)} custom-call(f32[8,16,2,2,8,128]{5,4,3,2,1,0:T(8,128)S(1)} %bitcast.9, f32[8,8,128]{2,1,0:T(8,128)S(1)} %get-tuple-element.10.tans), custom_call_target="tpu_custom_call" | custom-call | flops 10000000 | bytes 5242880 | tf_op jit(solution)/shard_map/third/pallas_call | solution.py:295
Async XLA Ops:
  4.7 52.9 %copy-start = (f32[2,128]{1,0:T(2,128)S(1)}, f32[2,128]{1,0:T(2,128)}, u32[]{:S(2)}) copy-start(f32[2,128]{1,0:T(2,128)} %angle.1) | copy-start | bytes 3076

commit v6 on v5

--- a/solution.py
+++ b/solution.py
@@ -8,13 +8,14 @@
 from jax.sharding import PartitionSpec as P
 
 AXES = ("x", "c", "z", "y")
-ORDER = ("y", "z", "x", "c")
+ORDER = ("z", "y", "x", "c")
 VMEM = pltpu.VMEM
 SMEM = pltpu.SMEM
 HOME = (2, 8, 32, 8, 128)
 SENT = (8, 16, 3, 2, 8, 128)
 AWAY = (8, 16, 2, 2, 8, 128)
 LANES, ROWS, BLOCK, MIDDLE = range(4)
+PLACE = [g for a in ORDER for g in {"x": [BLOCK] * 2, "c": [BLOCK], "y": [MIDDLE] * 2, "z": [MIDDLE] * 2}[a]]
 
 
 def fit(fn, terms, most=5.77):
@@ -202,9 +203,11 @@
         cos, sin = turn_factors(turn, 1)
         for g in range(1, 4):
             tans[4 + g] = sin[g] / cos[g]
-        pair = cos[ROWS] * cos[BLOCK] * cos[MIDDLE]
+        pair = cos[ROWS] * cos[BLOCK]
         rest = pair * pair * pair * cos[BLOCK]
-        store_tables(cos, sin, rest, (MIDDLE, BLOCK, BLOCK, BLOCK, ROWS), next_lanes, next_rows)
+        for g in PLACE[:3]:
+            rest = rest * cos[g]
+        store_tables(cos, sin, rest, (*PLACE[3:], ROWS), next_lanes, next_rows)
 
     def prepare(b, block, at):
         if not at:
@@ -231,20 +234,20 @@
 
 
 def second_kernel(state, angle, tans, lanes, rows, out, held, even, odd):
-    block0, middle0, middle1 = tans[BLOCK], tans[MIDDLE], tans[4 + MIDDLE]
+    tans0, tans1 = ([tans[4 * layer + g] for g in PLACE] for layer in range(2))
     turned = jnp.broadcast_to(angle[1:2], (8, 128))
 
     @pl.loop(0, 32, unroll=4)
     def _(j):
         for p in range(2):
-            tiles = rotate_all([state[i, j >> 1, p, j & 1] for i in range(8)], [middle0] * 3)
+            tiles = rotate_all([state[i, j >> 1, p, j & 1] for i in range(8)], tans0[:3])
             for i in range(8):
                 held[p, i, j] = tiles[i]
 
     def prepare(b, block, at):
         for r in range(2):
             re, im = (
-                rotate_all([held[p, b, 2 * q + r] for q in range(16)], [middle0, block0, block0, block0])
+                rotate_all([held[p, b, 2 * q + r] for q in range(16)], tans0[3:])
                 for p in range(2)
             )
             for q in range(16):
@@ -260,7 +263,7 @@
     @pl.loop(0, 32, unroll=4)
     def _(j):
         for p in range(2):
-            tiles = rotate_all([held[p, i, j] for i in range(8)], [middle1] * 3)
+            tiles = rotate_all([held[p, i, j] for i in range(8)], tans1[:3])
             for i in range(8):
                 out[i, j >> 1, p, j & 1] = tiles[i]
 

time: 98.2 us -> 97.8 us (level)
  no operation moved by 1% of the time
where the time goes in v6:
time: 97.8 us; the launch traced here: 97.6 us
  blocking collectives  87.3 us (89%)
  Pallas kernels  10.2 us (10%)
    all_to_all x2, blocking collectives, exchange(): flat = lax.all_to_all(state.reshape(128, -1, 128), ORDER, 0, 0, tiled=True)  87.3 us
    pallas_call x3, Pallas kernels, call(): pl.pallas_call(kernel, out_shape=[jax.ShapeDtypeStruct(s, d) for s, d in...  10.2 us

profile of v6, /device:TPU:1, one launch (start us, length us, event | category | flops | bytes accessed | tf_op | source)
XLA Modules:
  0.0 97.6 jit_solution(17165771010732314010)
XLA Ops:
  0.0 4.6 %first.1 = (f32[8,16,3,2,8,128]{5,4,3,2,1,0:T(8,128)S(1)}, f32[8,8,128]{2,1,0:T(8,128)S(1)}, bf16[256,256]{1,0:T(8,128)(2,1)S(1)}, bf16[256,768]{1,0:T(8,128)(2,1)S(1)}) custom-call(f32[2,4]{1,0:T(2,128)} %turn_hbm.1, f32[2,128]{1,0:T(2,128)} %angle.1, f32[2,8,32,8,128]{4,3,2,1,0:T(8,128)} %bitcast.11, f32[8,16,2,8,128]{4,3,2,1,0:T(8,128)} %bitcast.12), custom_call_target="tpu_custom_call" | custom-call | flops 20000000 | bytes 5242880 | tf_op jit(solution)/shard_map/first/pallas_call | solution.py:298
  4.7 0.0 copy-start
  4.7 52.8 %all_to_all.10 = f32[128,48,128]{2,1,0:T(8,128)S(1)} all-to-all(f32[128,48,128]{2,1,0:T(8,128)S(1)} %bitcast.10), channel_id=1, replica_groups=mesh['x'=4,'c'=2,'z'=4,'y'=4] {'z','y','x','c'}, dimensions={0} | all-to-all | bytes 6291456 | tf_op jit(solution)/shard_map/all_to_all | solution.py:311
  57.4 0.0 copy-done
  57.4 3.6 %second.1 = f32[8,16,2,2,8,128]{5,4,3,2,1,0:T(8,128)S(1)} custom-call(f32[8,16,3,2,8,128]{5,4,3,2,1,0:T(8,128)S(1)} %bitcast.7, f32[2,128]{1,0:T(2,128)S(1)} %copy-done, f32[8,8,128]{2,1,0:T(8,128)S(1)} %get-tuple-element.10.tans, bf16[256,256]{1,0:T(8,128)(2,1)S(1)} %get-tuple-element.11.lanes, bf16[256,768]{1,0:T(8,128)(2,1)S(1)} %get-tuple-element.12.rows), custom_call_target="tpu_custom_call" | custom-call | flops 20000000 | bytes 5242880 | tf_op jit(solution)/shard_map/second/pallas_call | solution.py:298
  61.1 34.6 %all_to_all.11 = f32[128,32,128]{2,1,0:T(8,128)S(1)} all-to-all(f32[128,32,128]{2,1,0:T(8,128)S(1)} %bitcast.8), channel_id=1, replica_groups=mesh['x'=4,'c'=2,'z'=4,'y'=4] {'z','y','x','c'}, dimensions={0} | all-to-all | bytes 4194304 | tf_op jit(solution)/shard_map/all_to_all | solution.py:311
  95.6 2.0 %third.1 = f32[2,8,32,8,128]{4,3,2,1,0:T(8,128)} custom-call(f32[8,16,2,2,8,128]{5,4,3,2,1,0:T(8,128)S(1)} %bitcast.9, f32[8,8,128]{2,1,0:T(8,128)S(1)} %get-tuple-element.10.tans), custom_call_target="tpu_custom_call" | custom-call | flops 10000000 | bytes 5242880 | tf_op jit(solution)/shard_map/third/pallas_call | solution.py:298
Async XLA Ops:
  4.7 52.8 %copy-start = (f32[2,128]{1,0:T(2,128)S(1)}, f32[2,128]{1,0:T(2,128)}, u32[]{:S(2)}) copy-start(f32[2,128]{1,0:T(2,128)} %angle.1) | copy-start | bytes 3076

commit v7 on v6

--- a/solution.py
+++ b/solution.py
@@ -8,7 +8,7 @@
 from jax.sharding import PartitionSpec as P
 
 AXES = ("x", "c", "z", "y")
-ORDER = ("z", "y", "x", "c")
+ORDER = ("z", "c", "y", "x")
 VMEM = pltpu.VMEM
 SMEM = pltpu.SMEM
 HOME = (2, 8, 32, 8, 128)
@@ -225,7 +225,7 @@
 
     in_step(prepare, finish, (even, odd))
 
-    @pl.loop(0, 32, unroll=4)
+    @pl.loop(0, 32, unroll=8)
     def _(j):
         for p in range(2):
             tiles = rotate_all([state[p, i, j] for i in range(8)], [block0] * 3)
@@ -237,7 +237,7 @@
     tans0, tans1 = ([tans[4 * layer + g] for g in PLACE] for layer in range(2))
     turned = jnp.broadcast_to(angle[1:2], (8, 128))
 
-    @pl.loop(0, 32, unroll=4)
+    @pl.loop(0, 32, unroll=8)
     def _(j):
         for p in range(2):
             tiles = rotate_all([state[i, j >> 1, p, j & 1] for i in range(8)], tans0[:3])
@@ -260,7 +260,7 @@
 
     in_step(prepare, finish, (even, odd))
 
-    @pl.loop(0, 32, unroll=4)
+    @pl.loop(0, 32, unroll=8)
     def _(j):
         for p in range(2):
             tiles = rotate_all([held[p, i, j] for i in range(8)], tans1[:3])
@@ -273,7 +273,7 @@
     copies = []
     for p in range(2):
 
-        @pl.loop(0, 32, unroll=4)
+        @pl.loop(0, 32, unroll=8)
         def _(j):
             tiles = rotate_all([state[i, j >> 1, p, j & 1] for i in range(8)], [block] * 3)
             for i in range(8):

time: 97.8 us -> 96.8 us (0.990)
  no operation moved by 1% of the time
where the time goes in v7:
time: 96.8 us; the launch traced here: 96.6 us
  blocking collectives  86.5 us (89%)
  Pallas kernels  10.1 us (10%)
    all_to_all x2, blocking collectives, exchange(): flat = lax.all_to_all(state.reshape(128, -1, 128), ORDER, 0, 0, tiled=True)  86.5 us
    pallas_call x3, Pallas kernels, call(): pl.pallas_call(kernel, out_shape=[jax.ShapeDtypeStruct(s, d) for s, d in...  10.1 us

profile of v7, /device:TPU:1, one launch (start us, length us, event | category | flops | bytes accessed | tf_op | source)
XLA Modules:
  0.0 96.6 jit_solution(2607479707644378078)
XLA Ops:
  0.0 4.6 %first.1 = (f32[8,16,3,2,8,128]{5,4,3,2,1,0:T(8,128)S(1)}, f32[8,8,128]{2,1,0:T(8,128)S(1)}, bf16[256,256]{1,0:T(8,128)(2,1)S(1)}, bf16[256,768]{1,0:T(8,128)(2,1)S(1)}) custom-call(f32[2,4]{1,0:T(2,128)} %turn_hbm.1, f32[2,128]{1,0:T(2,128)} %angle.1, f32[2,8,32,8,128]{4,3,2,1,0:T(8,128)} %bitcast.11, f32[8,16,2,8,128]{4,3,2,1,0:T(8,128)} %bitcast.12), custom_call_target="tpu_custom_call" | custom-call | flops 20000000 | bytes 5242880 | tf_op jit(solution)/shard_map/first/pallas_call | solution.py:298
  4.6 0.0 copy-start
  4.6 52.2 %all_to_all.10 = f32[128,48,128]{2,1,0:T(8,128)S(1)} all-to-all(f32[128,48,128]{2,1,0:T(8,128)S(1)} %bitcast.10), channel_id=1, replica_groups=mesh['x'=4,'c'=2,'z'=4,'y'=4] {'z','c','y','x'}, dimensions={0} | all-to-all | bytes 6291456 | tf_op jit(solution)/shard_map/all_to_all | solution.py:311
  56.9 0.0 copy-done
  56.9 3.6 %second.1 = f32[8,16,2,2,8,128]{5,4,3,2,1,0:T(8,128)S(1)} custom-call(f32[8,16,3,2,8,128]{5,4,3,2,1,0:T(8,128)S(1)} %bitcast.7, f32[2,128]{1,0:T(2,128)S(1)} %copy-done, f32[8,8,128]{2,1,0:T(8,128)S(1)} %get-tuple-element.10.tans, bf16[256,256]{1,0:T(8,128)(2,1)S(1)} %get-tuple-element.11.lanes, bf16[256,768]{1,0:T(8,128)(2,1)S(1)} %get-tuple-element.12.rows), custom_call_target="tpu_custom_call" | custom-call | flops 20000000 | bytes 5242880 | tf_op jit(solution)/shard_map/second/pallas_call | solution.py:298
  60.4 34.3 %all_to_all.11 = f32[128,32,128]{2,1,0:T(8,128)S(1)} all-to-all(f32[128,32,128]{2,1,0:T(8,128)S(1)} %bitcast.8), channel_id=1, replica_groups=mesh['x'=4,'c'=2,'z'=4,'y'=4] {'z','c','y','x'}, dimensions={0} | all-to-all | bytes 4194304 | tf_op jit(solution)/shard_map/all_to_all | solution.py:311
  94.7 1.9 %third.1 = f32[2,8,32,8,128]{4,3,2,1,0:T(8,128)} custom-call(f32[8,16,2,2,8,128]{5,4,3,2,1,0:T(8,128)S(1)} %bitcast.9, f32[8,8,128]{2,1,0:T(8,128)S(1)} %get-tuple-element.10.tans), custom_call_target="tpu_custom_call" | custom-call | flops 10000000 | bytes 5242880 | tf_op jit(solution)/shard_map/third/pallas_call | solution.py:298
Async XLA Ops:
  4.6 52.2 %copy-start = (f32[2,128]{1,0:T(2,128)S(1)}, f32[2,128]{1,0:T(2,128)}, u32[]{:S(2)}) copy-start(f32[2,128]{1,0:T(2,128)} %angle.1) | copy-start | bytes 3076

commit v8 on v7

--- a/solution.py
+++ b/solution.py
@@ -8,7 +8,7 @@
 from jax.sharding import PartitionSpec as P
 
 AXES = ("x", "c", "z", "y")
-ORDER = ("z", "c", "y", "x")
+ORDER = ("y", "c", "z", "x")
 VMEM = pltpu.VMEM
 SMEM = pltpu.SMEM
 HOME = (2, 8, 32, 8, 128)

time: 96.8 us -> 96.2 us (level)
  no operation moved by 1% of the time
where the time goes in v8:
time: 96.2 us; the launch traced here: 96 us
  blocking collectives  85.9 us (89%)
  Pallas kernels  10.1 us (10%)
    all_to_all x2, blocking collectives, exchange(): flat = lax.all_to_all(state.reshape(128, -1, 128), ORDER, 0, 0, tiled=True)  85.9 us
    pallas_call x3, Pallas kernels, call(): pl.pallas_call(kernel, out_shape=[jax.ShapeDtypeStruct(s, d) for s, d in...  10.1 us

profile of v8, /device:TPU:1, one launch (start us, length us, event | category | flops | bytes accessed | tf_op | source)
XLA Modules:
  0.0 96.0 jit_solution(17244811430755700725)
XLA Ops:
  0.0 4.6 %first.1 = (f32[8,16,3,2,8,128]{5,4,3,2,1,0:T(8,128)S(1)}, f32[8,8,128]{2,1,0:T(8,128)S(1)}, bf16[256,256]{1,0:T(8,128)(2,1)S(1)}, bf16[256,768]{1,0:T(8,128)(2,1)S(1)}) custom-call(f32[2,4]{1,0:T(2,128)} %turn_hbm.1, f32[2,128]{1,0:T(2,128)} %angle.1, f32[2,8,32,8,128]{4,3,2,1,0:T(8,128)} %bitcast.11, f32[8,16,2,8,128]{4,3,2,1,0:T(8,128)} %bitcast.12), custom_call_target="tpu_custom_call" | custom-call | flops 20000000 | bytes 5242880 | tf_op jit(solution)/shard_map/first/pallas_call | solution.py:298
  4.6 0.0 copy-start
  4.6 51.8 %all_to_all.10 = f32[128,48,128]{2,1,0:T(8,128)S(1)} all-to-all(f32[128,48,128]{2,1,0:T(8,128)S(1)} %bitcast.10), channel_id=1, replica_groups=mesh['x'=4,'c'=2,'z'=4,'y'=4] {'y','c','z','x'}, dimensions={0} | all-to-all | bytes 6291456 | tf_op jit(solution)/shard_map/all_to_all | solution.py:311
  56.4 0.0 copy-done
  56.5 3.6 %second.1 = f32[8,16,2,2,8,128]{5,4,3,2,1,0:T(8,128)S(1)} custom-call(f32[8,16,3,2,8,128]{5,4,3,2,1,0:T(8,128)S(1)} %bitcast.7, f32[2,128]{1,0:T(2,128)S(1)} %copy-done, f32[8,8,128]{2,1,0:T(8,128)S(1)} %get-tuple-element.10.tans, bf16[256,256]{1,0:T(8,128)(2,1)S(1)} %get-tuple-element.11.lanes, bf16[256,768]{1,0:T(8,128)(2,1)S(1)} %get-tuple-element.12.rows), custom_call_target="tpu_custom_call" | custom-call | flops 20000000 | bytes 5242880 | tf_op jit(solution)/shard_map/second/pallas_call | solution.py:298
  60.0 34.1 %all_to_all.11 = f32[128,32,128]{2,1,0:T(8,128)S(1)} all-to-all(f32[128,32,128]{2,1,0:T(8,128)S(1)} %bitcast.8), channel_id=1, replica_groups=mesh['x'=4,'c'=2,'z'=4,'y'=4] {'y','c','z','x'}, dimensions={0} | all-to-all | bytes 4194304 | tf_op jit(solution)/shard_map/all_to_all | solution.py:311
  94.1 1.9 %third.1 = f32[2,8,32,8,128]{4,3,2,1,0:T(8,128)} custom-call(f32[8,16,2,2,8,128]{5,4,3,2,1,0:T(8,128)S(1)} %bitcast.9, f32[8,8,128]{2,1,0:T(8,128)S(1)} %get-tuple-element.10.tans), custom_call_target="tpu_custom_call" | custom-call | flops 10000000 | bytes 5242880 | tf_op jit(solution)/shard_map/third/pallas_call | solution.py:298
Async XLA Ops:
  4.6 51.8 %copy-start = (f32[2,128]{1,0:T(2,128)S(1)}, f32[2,128]{1,0:T(2,128)}, u32[]{:S(2)}) copy-start(f32[2,128]{1,0:T(2,128)} %angle.1) | copy-start | bytes 3076
